TPU v7x, 512 devices: a whole 4x4x16 slice. The times are simulated.
512 devices in a mesh: bytes: 16 (over z), ctx: 8 (over x, core), tp: 4 (over y).
Axes of the slice: x: 4, y: 4, z: 16, core: 2. Of those that a mesh axis runs over, the one named last changes fastest.
Arguments:
- byte_values_sequence: int32 [24576], P(('bytes', 'ctx')), may hold values from 0 to 255
- offsets: int32 [24576], P(('bytes', 'ctx')), may hold values from 0 to 168, as said below
- byte_table: bfloat16 [256, 1024], replicated, may hold values from -6 to 6
- byte_query: bfloat16 [1024, 1024], P(None, 'tp'), may hold values from -1 to 1
- byte_key: bfloat16 [1024, 1024], P(None, 'tp'), may hold values from -16 to 16
- byte_value: bfloat16 [1024, 1024], P(None, 'tp'), may hold values from -0.1875 to 0.1875
- latent_query: bfloat16 [1024, 4096], P(None, ('ctx', 'tp')), may hold values from -1 to 1
- latent_key: bfloat16 [1024, 4096], P(None, ('ctx', 'tp')), may hold values from -16 to 16
- latent_value: bfloat16 [1024, 4096], P(None, ('ctx', 'tp')), may hold values from -0.1875 to 0.1875
- decode_weight: bfloat16 [4096, 1024], P(('ctx', 'tp')), may hold values from -1 to 1
Outputs:
- byte_output: bfloat16 [24576, 1024], P(('bytes', 'ctx'), 'tp')
Inputs may be any that keep to these rules, and one draw needn't show every extreme that they name: offsets[i] is 0 where a patch starts and offsets[i - 1] + 1 elsewhere; the first byte of every device's 192 bytes starts a patch; one device's bytes hold 24 to 72 patch starts and the bytes of the devices of one index of bytes hold at most 384; both most values are reached in every draw.
All inputs are finite; a program needn't handle non-finite values.
Results may differ from a plain program's by a relative error of at most 0.017.
Values may be sent and summed in bfloat16 or wider, within the bound.
No kernel may reach another device: no remote copies, remote signals or barrier semaphores. Data moves between devices by JAX's collectives and lax.ppermute only.
A program may use at most 64 MiB of HBM per device.

v0:
```python
import math

import jax
import jax.numpy as jnp
from jax import lax
from jax.experimental import pallas as pl
from jax.experimental.pallas import tpu as pltpu
from jax.sharding import PartitionSpec as P

DB = 1024
HEADS_B = 16
HEAD_L = 128
SLOTS = 72
ROWS = 80
GROUP = 384
KVROWS = 392
SPAN = 4
EPSILON = 1e-06
NEGATIVE = -1e30
F32 = jnp.float32
BF16 = jnp.bfloat16

VMEM = pl.BlockSpec(memory_space=pltpu.VMEM)
SMEM = pl.BlockSpec(memory_space=pltpu.SMEM)


def iota(shape, dim):
    return lax.broadcasted_iota(jnp.int32, shape, dim)


def dot(a, b):
    return jnp.dot(a, b, preferred_element_type=F32)


def dot_nt(a, b):
    return lax.dot_general(a, b, (((1,), (1,)), ((), ())), preferred_element_type=F32)


def dot_tn(a, b):
    return lax.dot_general(a, b, (((0,), (0,)), ((), ())), preferred_element_type=F32)


def table_kernel(table_ref, wq_ref, wk_ref, wv_ref, out_ref):
    embedded = table_ref[...].astype(F32)
    scale = lax.rsqrt(jnp.mean(embedded * embedded, axis=-1, keepdims=True) + EPSILON)
    normed = (embedded * scale).astype(BF16)
    for k, w_ref in enumerate((wq_ref, wk_ref, wv_ref)):
        out_ref[:, 256 * k : 256 * (k + 1)] = dot(normed, w_ref[...]).astype(BF16)


def byte_kernel(block_ref, ids_ref, earlier_ref, offsets_ref, table_ref, enc_ref, member_ref, pay_ref):
    n = ids_ref.shape[1]
    vocab = table_ref.shape[0]
    width = enc_ref.shape[1]
    onehot = (iota((vocab, n), 0) == ids_ref[...]).astype(F32).astype(BF16)
    onehot_e = (iota((vocab, n), 0) == earlier_ref[...]).astype(F32).astype(BF16)
    own = dot_tn(onehot, table_ref[...]).astype(BF16)
    before = dot_tn(onehot_e, table_ref[:, width:]).astype(BF16)
    queries = own[:, :width]
    keys = jnp.concatenate([before[:, :width], own[:, width : 2 * width]], axis=0)
    values = jnp.concatenate([before[:, width:], own[:, 2 * width :]], axis=0)
    query_pos = iota((n, 2 * n), 0)
    key_pos = iota((n, 2 * n), 1)
    first = jnp.where(block_ref[0] > 0, 0, n)
    allowed = (key_pos > query_pos) & (key_pos <= query_pos + n) & (key_pos >= first)
    head = 64
    encoded = jnp.zeros((n, width), F32)
    for h in range(width // head):
        column = iota((1, width), 1)
        mine = ((column >= h * head) & (column < (h + 1) * head)).astype(F32).astype(BF16)
        scores = dot_nt(queries * mine, keys) * (1.0 / math.sqrt(head))
        scores = jnp.where(allowed, scores, NEGATIVE)
        weights = jnp.exp(scores - jnp.max(scores, axis=-1, keepdims=True))
        totals = jnp.sum(weights, axis=-1, keepdims=True)
        encoded = encoded + dot(weights.astype(BF16), values * mine) / totals
    encoded = encoded.astype(BF16)
    enc_ref[...] = encoded
    starts = (offsets_ref[...] == 0).astype(F32)
    upto = (iota((n, n), 0) <= iota((n, n), 1)).astype(F32).astype(BF16)
    running = dot(jnp.broadcast_to(starts, (8, n)).astype(BF16), upto)[0:1]
    patch = running.astype(jnp.int32) - 1
    members = (iota((ROWS, n), 0) == patch).astype(F32)
    member_ref[...] = members.astype(BF16)
    lengths = jnp.sum(members, axis=1, keepdims=True)
    pooled = dot(members.astype(BF16), encoded) / jnp.maximum(lengths, 1.0)
    count = jnp.sum(starts, axis=1, keepdims=True)
    payload = jnp.where(iota((ROWS, width), 0) == SLOTS, count, pooled).astype(BF16)
    for i in range(pay_ref.shape[0]):
        pay_ref[i] = payload


def latent_kernel(core_ref, own_ref, other_ref, wq_ref, wk_ref, wv_ref, q_ref, kv_ref, place_ref):
    blocks = own_ref.shape[0] // 4
    slots = 2 * blocks * ROWS
    is_odd = (core_ref[0] > 0).astype(F32)
    refs = [own_ref] * blocks + [other_ref] * blocks
    here = [r[4 * (k % blocks)][SLOTS : SLOTS + 1, 0:1].astype(F32) for k, r in enumerate(refs)]
    slot = iota((1, slots), 1)
    place = jnp.full((1, slots), -1.0, F32)
    total = jnp.zeros((1, 1), F32)
    for c in range(blocks):
        own, other = here[c], here[blocks + c]
        for k, filled, ahead in ((c, own, total + other * is_odd), (blocks + c, other, total + own * (1.0 - is_odd))):
            order = (slot - ROWS * k).astype(F32)
            place = jnp.where((order >= 0.0) & (order < filled), order + ahead, place)
        total = total + own + other
    place = place.astype(jnp.int32)
    place_ref[...] = jnp.broadcast_to(place, place_ref.shape)
    queries, keys, values = [], [], []
    for k, r in enumerate(refs):
        parts = [r[4 * (k % blocks) + t].astype(F32) for t in range(4)]
        square = sum(jnp.sum(p * p, axis=-1, keepdims=True) for p in parts)
        scale = lax.rsqrt(square * (1.0 / DB) + EPSILON)
        latent = jnp.concatenate([(p * scale).astype(BF16) for p in parts], axis=1)
        queries.append(dot(latent, wq_ref[...]).astype(BF16))
        keys.append(dot(latent, wk_ref[...]).astype(BF16))
        values.append(dot(latent, wv_ref[...]).astype(BF16))
    pick = (iota((GROUP, slots), 0) == place).astype(F32).astype(BF16)
    q_ref[...] = dot(pick, jnp.concatenate(queries, axis=0)).astype(BF16)
    kv_ref[0:GROUP, 0:HEAD_L] = dot(pick, jnp.concatenate(keys, axis=0)).astype(BF16)
    value = dot(pick, jnp.concatenate(values, axis=0))
    largest = jnp.max(jnp.max(jnp.abs(value), axis=1, keepdims=True), axis=0, keepdims=True)
    power = jnp.clip(13.0 - jnp.ceil(jnp.log2(jnp.maximum(largest, 1e-35))), -20.0, 100.0)
    kv_ref[0:GROUP, HEAD_L:] = (value * jnp.exp2(power)).astype(BF16)
    high = total.astype(BF16).astype(F32)
    row = iota((KVROWS - GROUP, 2 * HEAD_L), 0)
    tail = jnp.where(row == 0, high, jnp.where(row == 1, total - high, jnp.where(row == 2, power, 0.0)))
    kv_ref[GROUP:, :] = tail.astype(BF16)


SCALE = 1.0 / (math.sqrt(HEAD_L) * math.log(2.0))


def attend_kernel(z_ref, q_ref, kv_ref, out_ref, m_ref, l_ref, acc_ref):
    m_ref[...] = jnp.full(m_ref.shape, NEGATIVE, F32)
    l_ref[...] = jnp.zeros(l_ref.shape, F32)
    acc_ref[...] = jnp.zeros(acc_ref.shape, F32)
    z = z_ref[0]
    for tile in range(kv_ref.shape[0] // SPAN):

        @pl.when(z >= tile * SPAN)
        def _(tile=tile):
            codes, scores = [], []
            for b in range(tile * SPAN, (tile + 1) * SPAN):
                filled = kv_ref[b, GROUP : GROUP + 1, 0:1].astype(F32) + kv_ref[b, GROUP + 1 : GROUP + 2, 0:1].astype(F32)
                spot = iota((1, GROUP), 1)
                past = jnp.where(spot.astype(F32) < filled, -1, GROUP)
                codes.append(jnp.where(z > b, past, jnp.where(z == b, spot, GROUP)))
                scores.append(dot_nt(q_ref[...], kv_ref[b, 0:GROUP, 0:HEAD_L]))
            code = jnp.concatenate(codes, axis=1)
            score = jnp.concatenate(scores, axis=1) * SCALE
            score = jnp.where(code <= iota((GROUP, 1), 0), score, NEGATIVE)
            old = m_ref[:, 0:1]
            highest = jnp.maximum(old, jnp.max(score, axis=-1, keepdims=True))
            factor = jnp.exp2(old - highest)
            weights = jnp.exp2(score - highest)
            m_ref[...] = jnp.broadcast_to(highest, m_ref.shape)
            l_ref[...] = l_ref[...] * factor + jnp.sum(weights, axis=-1, keepdims=True)
            weights = weights.astype(BF16)
            mixed = acc_ref[...] * factor
            for k in range(SPAN):
                b = tile * SPAN + k
                back = jnp.exp2(-kv_ref[b, GROUP + 2 : GROUP + 3, 0:1].astype(F32))
                mixed = mixed + dot(weights[:, GROUP * k : GROUP * (k + 1)], kv_ref[b, 0:GROUP, HEAD_L:]) * back
            acc_ref[...] = mixed

    out_ref[...] = (acc_ref[...] / l_ref[...]).astype(BF16)


def share_kernel(mixed_ref, place_ref, w_ref, own_ref, other_ref):
    slots = place_ref.shape[1]
    blocks = slots // (2 * ROWS)
    pick = (iota((GROUP, slots), 0) == place_ref[0:1]).astype(F32).astype(BF16)
    spread = dot_tn(pick, mixed_ref[...]).astype(BF16)
    width = own_ref.shape[2]
    for t in range(4):
        part = dot(spread, w_ref[:, width * t : width * (t + 1)]).astype(BF16)
        for c in range(2 * blocks):
            dest_ref = own_ref if c < blocks else other_ref
            dest_ref[4 * (c % blocks) + t] = part[ROWS * c : ROWS * c + SLOTS]


def output_kernel(got_ref, enc_ref, member_ref, out_ref):
    decoded = got_ref[0].astype(F32)
    for h in range(1, got_ref.shape[0]):
        decoded = decoded + got_ref[h].astype(F32)
    decoded = jnp.concatenate([decoded, jnp.zeros((ROWS - SLOTS, decoded.shape[1]), F32)], axis=0)
    high = decoded.astype(BF16)
    low = (decoded - high.astype(F32)).astype(BF16)
    members = member_ref[...]
    out_ref[...] = (enc_ref[...].astype(F32) + dot_tn(members, high) + dot_tn(members, low)).astype(BF16)


def call(kernel, shapes, specs, *args, scratch=()):
    single = not isinstance(shapes, list)
    structs = [jax.ShapeDtypeStruct(s, d) for s, d in ([shapes] if single else shapes)]
    return pl.pallas_call(
        kernel,
        out_shape=structs[0] if single else structs,
        in_specs=specs,
        out_specs=VMEM if single else [VMEM] * len(structs),
        scratch_shapes=scratch,
    )(*args)


def scalar(value):
    return value.astype(jnp.int32).reshape(1)


def swap_cores(value):
    return lax.ppermute(value, "core", [(0, 1), (1, 0)])


def exchange(value):
    return lax.all_to_all(value, ("x", "tp"), split_axis=0, concat_axis=0, tiled=True)


def gather_keys(kv):
    size = lax.axis_size("bytes")
    got = lax.all_gather(kv.astype(jnp.float16), "bytes", axis=0, tiled=True)
    return got.astype(BF16).reshape(size, *kv.shape)


def per_device(ids, offsets, byte_table, byte_query, byte_key, byte_value, latent_query, latent_key, latent_value, decode_weight):
    n = ids.shape[0]
    width = byte_query.shape[1]
    ring = ("bytes", "x", "core")
    plane = lax.axis_size(("x", "tp"))
    earlier = lax.ppermute(ids, ring, [(i, i + 1) for i in range(lax.axis_size(ring) - 1)])
    table = call(table_kernel, ((byte_table.shape[0], 3 * width), BF16), [VMEM] * 4, byte_table, byte_query, byte_key, byte_value)
    encoded, members, payload = call(
        byte_kernel,
        [((n, width), BF16), ((ROWS, n), BF16), ((plane, ROWS, width), BF16)],
        [SMEM] + [VMEM] * 4,
        scalar(lax.axis_index(ring)), ids.reshape(1, n), earlier.reshape(1, n), offsets.reshape(1, n), table,
    )
    own = exchange(payload)
    other = swap_cores(own)
    queries, kv, place = call(
        latent_kernel,
        [((GROUP, HEAD_L), BF16), ((KVROWS, 2 * HEAD_L), BF16), ((8, 2 * ROWS * plane // 4), jnp.int32)],
        [SMEM] + [VMEM] * 5,
        scalar(lax.axis_index("core")), own, other, latent_query, latent_key, latent_value,
    )
    mixed = call(
        attend_kernel,
        ((GROUP, HEAD_L), BF16),
        [SMEM] + [VMEM] * 2,
        scalar(lax.axis_index("bytes")), queries, gather_keys(kv),
        scratch=[pltpu.VMEM((GROUP, HEAD_L), F32)] * 3,
    )
    shape = ((plane, SLOTS, width), BF16)
    mine, theirs = call(share_kernel, [shape, shape], [VMEM] * 3, mixed, place, decode_weight)
    shares = (mine.astype(F32) + swap_cores(theirs).astype(F32)).astype(BF16)
    return call(output_kernel, ((n, width), BF16), [VMEM] * 3, exchange(shares), encoded, members)


def solution(mesh):
    sizes = mesh.shape
    finer = jax.sharding.Mesh(
        mesh.devices.reshape(sizes["bytes"], sizes["ctx"] // 2, 2, sizes["tp"]), ("bytes", "x", "core", "tp")
    )
    rows, heads = ("bytes", "x", "core"), ("x", "core", "tp")
    return jax.shard_map(
        per_device,
        mesh=finer,
        in_specs=(
            P(rows),
            P(rows),
            P(),
            P(None, "tp"),
            P(None, "tp"),
            P(None, "tp"),
            P(None, heads),
            P(None, heads),
            P(None, heads),
            P(heads, None),
        ),
        out_specs=P(rows, "tp"),
        check_vma=False,
    )
```

profile of v0, /device:TPU:1, one launch (start us, length us, event | category | flops | bytes accessed | tf_op | source)
XLA Modules:
  0.0 132.1 jit_solution(9119673854518172948)
XLA Ops:
  0.0 4.5 %collective-permute-start = (s32[192]{0:T(256)}, s32[192]{0:T(256)S(1)}, u32[]{:S(2)}, u32[]{:S(2)}) collective-permute-start(s32[192]{0:T(256)} %param.10), channel_id=1, source_target_pairs={{0,4},{4,8},{8,12},{12,16},{16,20},{20,24},{24,28},{28,32},{32,36}... | collective-permute-start | bytes 2312 | tf_op jit(solution)/shard_map/ppermute | solution.py:229
  4.5 2.9 %shard_map.100.table_ref = bf16[256,768]{1,0:T(8,128)(2,1)} custom-call(bf16[256,1024]{1,0:T(8,128)(2,1)} %table_ref.1, bf16[1024,256]{1,0:T(8,128)(2,1)} %wq_ref.2, bf16[1024,256]{1,0:T(8,128)(2,1)} %wk_ref.2, bf16[1024,256]{1,0:T(8,128)(2,1)} %wv_ref.2), custom_call_target="tpu_custom_call" | custom-call | tf_op jit(solution)/shard_map/pallas_call | solution.py:197
  7.4 1.5 %collective-permute-done = s32[192]{0:T(256)S(1)} collective-permute-done((s32[192]{0:T(256)}, s32[192]{0:T(256)S(1)}, u32[]{:S(2)}, u32[]{:S(2)}) %collective-permute-start) | collective-permute-done | bytes 800 | tf_op jit(solution)/shard_map/ppermute | solution.py:229
  9.0 0.0 copy-start.2
  9.0 0.6 copy-done.2
  9.5 3.6 %shard_map.101 = (bf16[192,256]{1,0:T(8,128)(2,1)}, bf16[80,192]{1,0:T(8,128)(2,1)}, bf16[16,80,256]{2,1,0:T(8,128)(2,1)}) custom-call(s32[1]{0:T(128)} %bitcast.2.block_ref, s32[1,192]{1,0:T(1,128)} %bitcast.8, s32[1,192]{1,0:T(1,128)} %bitcast.10, s32[1,192]{1,0:T(1,128)} %bitcast.9, bf16[256,768]{1,0:T(8,128)(2,1)} %shard_map.100.table_ref), custom_call_target="tpu_custom_call" | custom-call | tf_op jit(solution)/shard_map/pallas_call | solution.py:197
  13.1 17.6 %all_to_all.10.own_ref = bf16[16,80,256]{2,1,0:T(8,128)(2,1)S(1)} all-to-all(bf16[16,80,256]{2,1,0:T(8,128)(2,1)} %get-tuple-element.13), channel_id=1, replica_groups=mesh['bytes'=16,'x'=4,'core'=2,'tp'=4] {'x','tp'}, dimensions={0} | all-to-all | bytes 1310720 | tf_op jit(solution)/shard_map/all_to_all | solution.py:215
  30.7 0.0 copy-start
  30.7 3.3 %collective-permute-start.1 = (bf16[16,80,256]{2,1,0:T(8,128)(2,1)S(1)}, bf16[16,80,256]{2,1,0:T(8,128)(2,1)S(1)}, u32[]{:S(2)}, u32[]{:S(2)}) collective-permute-start(bf16[16,80,256]{2,1,0:T(8,128)(2,1)S(1)} %all_to_all.10.own_ref), channel_id=1, source_target_pairs={{0,4},{4,0},{1,5},{5,1},{2,6},{6,2},{3,7},{7,3},{8,12},{12,8},{9,1... | collective-permute-start | bytes 1966088 | tf_op jit(solution)/shard_map/ppermute | solution.py:211
  34.0 1.7 %collective-permute-done.1.other_ref = bf16[16,80,256]{2,1,0:T(8,128)(2,1)S(1)} collective-permute-done((bf16[16,80,256]{2,1,0:T(8,128)(2,1)S(1)}, bf16[16,80,256]{2,1,0:T(8,128)(2,1)S(1)}, u32[]{:S(2)}, u32[]{:S(2)}) %collective-permute-start.1) | collective-permute-done | bytes 655392 | tf_op jit(solution)/shard_map/ppermute | solution.py:211
  35.7 0.0 copy-start.1
  35.7 0.0 copy-done
  35.7 0.8 copy-done.1
  36.5 4.0 %shard_map.102 = (bf16[384,128]{1,0:T(8,128)(2,1)}, bf16[392,256]{1,0:T(8,128)(2,1)}, s32[8,640]{1,0:T(8,128)}) custom-call(s32[1]{0:T(128)} %bitcast.1.core_ref, bf16[16,80,256]{2,1,0:T(8,128)(2,1)} %copy-done, bf16[16,80,256]{2,1,0:T(8,128)(2,1)} %copy-done.1, bf16[1024,128]{1,0:T(8,128)(2,1)} %wq_ref.3, bf16[1024,128]{1,0:T(8,128)(2,1)} %wk_ref.3, ...), custom_call_target="tpu_custom_call" | custom-call | tf_op jit(solution)/shard_map/pallas_call | solution.py:197
  40.6 1.0 convert_element_type.15
  41.5 52.6 %all-gather.1 = f16[6272,256]{1,0:T(8,128)(2,1)S(1)} all-gather(f16[392,256]{1,0:T(8,128)(2,1)S(1)} %convert_element_type.15), channel_id=1, replica_groups=mesh['bytes'=16,'x'=4,'core'=2,'tp'=4] {'bytes'}, dimensions={0}, use_global_device_ids=true | all-gather | bytes 3411968 | tf_op jit(solution)/shard_map/all_gather | solution.py:220
  94.2 2.3 %convert_element_type.16 = bf16[6272,256]{1,0:T(8,128)(2,1)} convert(f16[6272,256]{1,0:T(8,128)(2,1)S(1)} %all-gather.1) | non-fusion elementwise | flops 1605632 | bytes 6422528 | tf_op jit(solution)/shard_map/convert_element_type | solution.py:221
  96.5 4.2 %shard_map.103.mixed_ref = bf16[384,128]{1,0:T(8,128)(2,1)} custom-call(s32[1]{0:T(128)} %bitcast.z_ref, bf16[384,128]{1,0:T(8,128)(2,1)} %get-tuple-element.14.q_ref, bf16[16,392,256]{2,1,0:T(8,128)(2,1)} %bitcast.7), custom_call_target="tpu_custom_call" | custom-call | tf_op jit(solution)/shard_map/pallas_call | solution.py:197
  100.7 2.7 %shard_map.104 = (bf16[16,72,256]{2,1,0:T(8,128)(2,1)}, bf16[16,72,256]{2,1,0:T(8,128)(2,1)}) custom-call(bf16[384,128]{1,0:T(8,128)(2,1)} %shard_map.103.mixed_ref, s32[8,640]{1,0:T(8,128)} %get-tuple-element.16.place_ref, bf16[128,1024]{1,0:T(8,128)(2,1)} %w_ref.1), custom_call_target="tpu_custom_call" | custom-call | tf_op jit(solution)/shard_map/pallas_call | solution.py:197
  103.3 9.0 %collective-permute-start.2 = (bf16[16,72,256]{2,1,0:T(8,128)(2,1)}, bf16[16,72,256]{2,1,0:T(8,128)(2,1)S(1)}, u32[]{:S(2)}, u32[]{:S(2)}) collective-permute-start(bf16[16,72,256]{2,1,0:T(8,128)(2,1)} %get-tuple-element.18), channel_id=1, source_target_pairs={{0,4},{4,0},{1,5},{5,1},{2,6},{6,2},{3,7},{7,3},{8,12},{12,8},{9,1... | collective-permute-start | bytes 1769480 | tf_op jit(solution)/shard_map/ppermute | solution.py:211
  112.3 1.8 %collective-permute-done.2 = bf16[16,72,256]{2,1,0:T(8,128)(2,1)S(1)} collective-permute-done((bf16[16,72,256]{2,1,0:T(8,128)(2,1)}, bf16[16,72,256]{2,1,0:T(8,128)(2,1)S(1)}, u32[]{:S(2)}, u32[]{:S(2)}) %collective-permute-start.2) | collective-permute-done | bytes 589856 | tf_op jit(solution)/shard_map/ppermute | solution.py:211
  114.1 1.2 add_convert_fusion
  115.3 14.7 %all_to_all.11.got_ref = bf16[16,72,256]{2,1,0:T(8,128)(2,1)} all-to-all(bf16[16,72,256]{2,1,0:T(8,128)(2,1)S(1)} %add_convert_fusion), channel_id=1, replica_groups=mesh['bytes'=16,'x'=4,'core'=2,'tp'=4] {'x','tp'}, dimensions={0} | all-to-all | bytes 1179648 | tf_op jit(solution)/shard_map/all_to_all | solution.py:215
  130.1 2.0 %shard_map.105 = bf16[192,256]{1,0:T(8,128)(2,1)} custom-call(bf16[16,72,256]{2,1,0:T(8,128)(2,1)} %all_to_all.11.got_ref, bf16[192,256]{1,0:T(8,128)(2,1)} %get-tuple-element.19.enc_ref, bf16[80,192]{1,0:T(8,128)(2,1)} %get-tuple-element.20.member_ref), custom_call_target="tpu_custom_call" | custom-call | tf_op jit(solution)/shard_map/pallas_call | solution.py:197
Async XLA Ops:
  0.0 9.0 %collective-permute-start = (s32[192]{0:T(256)}, s32[192]{0:T(256)S(1)}, u32[]{:S(2)}, u32[]{:S(2)}) collective-permute-start(s32[192]{0:T(256)} %param.10), channel_id=1, source_target_pairs={{0,4},{4,8},{8,12},{12,16},{16,20},{20,24},{24,28},{28,32},{32,36}... | collective-permute-start | bytes 2312 | tf_op jit(solution)/shard_map/ppermute | solution.py:229
  9.0 0.6 copy-start.2
  30.7 5.0 %copy-start = (bf16[16,80,256]{2,1,0:T(8,128)(2,1)}, bf16[16,80,256]{2,1,0:T(8,128)(2,1)S(1)}, u32[]{:S(2)}) copy-start(bf16[16,80,256]{2,1,0:T(8,128)(2,1)S(1)} %all_to_all.10.own_ref) | copy-start | bytes 1966084
  30.7 5.0 %collective-permute-start.1 = (bf16[16,80,256]{2,1,0:T(8,128)(2,1)S(1)}, bf16[16,80,256]{2,1,0:T(8,128)(2,1)S(1)}, u32[]{:S(2)}, u32[]{:S(2)}) collective-permute-start(bf16[16,80,256]{2,1,0:T(8,128)(2,1)S(1)} %all_to_all.10.own_ref), channel_id=1, source_target_pairs={{0,4},{4,0},{1,5},{5,1},{2,6},{6,2},{3,7},{7,3},{8,12},{12,8},{9,1... | collective-permute-start | bytes 1966088 | tf_op jit(solution)/shard_map/ppermute | solution.py:211
  35.7 0.8 copy-start.1
  103.3 10.8 %collective-permute-start.2 = (bf16[16,72,256]{2,1,0:T(8,128)(2,1)}, bf16[16,72,256]{2,1,0:T(8,128)(2,1)S(1)}, u32[]{:S(2)}, u32[]{:S(2)}) collective-permute-start(bf16[16,72,256]{2,1,0:T(8,128)(2,1)} %get-tuple-element.18), channel_id=1, source_target_pairs={{0,4},{4,0},{1,5},{5,1},{2,6},{6,2},{3,7},{7,3},{8,12},{12,8},{9,1... | collective-permute-start | bytes 1769480 | tf_op jit(solution)/shard_map/ppermute | solution.py:211
where the time goes:
time: 133 us; the launch traced here: 132 us
  blocking collectives  85 us (64%)
  Pallas kernels  19.4 us (15%)
  starting transfers between devices  16.7 us (13%)
  waiting for transfers between devices  5.06 us (4%)
  other arithmetic  4.51 us (3%)
  local copies, waits for them, and re-layouts  1.41 us (1%)
    all_gather x1, blocking collectives, gather_keys(): got = lax.all_gather(kv.astype(jnp.float16), 'bytes', axis=0, tiled=True)  52.6 us
    all_to_all x2, blocking collectives, exchange(): lax.all_to_all(value, ('x', 'tp'), split_axis=0, concat_axis=0, tiled=True)  32.4 us
    pallas_call x6, Pallas kernels, call(): pl.pallas_call(kernel, out_shape=structs[0] if single else structs, in_sp...  19.4 us
    ppermute x2, starting transfers between devices, swap_cores(): return lax.ppermute(value, 'core', [(0, 1), (1, 0)])  12.3 us
    ppermute x1, starting transfers between devices, per_device(): lax.ppermute(ids, ring, [(i, i + 1) for i in range(lax.axis_size(ring) -...  4.49 us
    ppermute x2, waiting for transfers between devices, swap_cores(): return lax.ppermute(value, 'core', [(0, 1), (1, 0)])  3.52 us
  transfers between devices with their start and end apart: 3, of which 3 were waited for; matrix products, arithmetic and copies ran while one was open for 0% of the time, Pallas kernels for 2%

commit v1 on v0

--- a/solution.py
+++ b/solution.py
@@ -11,7 +11,8 @@
 HEADS_B = 16
 HEAD_L = 128
 SLOTS = 72
-ROWS = 80
+ROWS = 72
+UNUSED = 1e9
 GROUP = 384
 KVROWS = 392
 SPAN = 4
@@ -83,8 +84,8 @@
     member_ref[...] = members.astype(BF16)
     lengths = jnp.sum(members, axis=1, keepdims=True)
     pooled = dot(members.astype(BF16), encoded) / jnp.maximum(lengths, 1.0)
-    count = jnp.sum(starts, axis=1, keepdims=True)
-    payload = jnp.where(iota((ROWS, width), 0) == SLOTS, count, pooled).astype(BF16)
+    empty = (lengths < 0.5) & (iota((ROWS, width), 1) == 0)
+    payload = jnp.where(empty, UNUSED, pooled).astype(BF16)
     for i in range(pay_ref.shape[0]):
         pay_ref[i] = payload
 
@@ -93,8 +94,17 @@
     blocks = own_ref.shape[0] // 4
     slots = 2 * blocks * ROWS
     is_odd = (core_ref[0] > 0).astype(F32)
-    refs = [own_ref] * blocks + [other_ref] * blocks
-    here = [r[4 * (k % blocks)][SLOTS : SLOTS + 1, 0:1].astype(F32) for k, r in enumerate(refs)]
+    weight = jnp.concatenate([wq_ref[...], wk_ref[...], wv_ref[...]], axis=1)
+    here, rows = [], []
+    for r in (own_ref, other_ref):
+        for k in range(blocks):
+            parts = [r[4 * k + t].astype(F32) for t in range(4)]
+            used = (parts[0][:, 0:1] < 0.1 * UNUSED).astype(F32)
+            here.append(jnp.sum(used, axis=0, keepdims=True))
+            square = sum(jnp.sum(p * p, axis=-1, keepdims=True) for p in parts)
+            scale = used * lax.rsqrt(square * (1.0 / DB) + EPSILON)
+            rows.append(jnp.concatenate([(p * scale).astype(BF16) for p in parts], axis=1))
+    made = dot(jnp.concatenate(rows, axis=0), weight).astype(BF16)
     slot = iota((1, slots), 1)
     place = jnp.full((1, slots), -1.0, F32)
     total = jnp.zeros((1, 1), F32)
@@ -106,19 +116,11 @@
         total = total + own + other
     place = place.astype(jnp.int32)
     place_ref[...] = jnp.broadcast_to(place, place_ref.shape)
-    queries, keys, values = [], [], []
-    for k, r in enumerate(refs):
-        parts = [r[4 * (k % blocks) + t].astype(F32) for t in range(4)]
-        square = sum(jnp.sum(p * p, axis=-1, keepdims=True) for p in parts)
-        scale = lax.rsqrt(square * (1.0 / DB) + EPSILON)
-        latent = jnp.concatenate([(p * scale).astype(BF16) for p in parts], axis=1)
-        queries.append(dot(latent, wq_ref[...]).astype(BF16))
-        keys.append(dot(latent, wk_ref[...]).astype(BF16))
-        values.append(dot(latent, wv_ref[...]).astype(BF16))
     pick = (iota((GROUP, slots), 0) == place).astype(F32).astype(BF16)
-    q_ref[...] = dot(pick, jnp.concatenate(queries, axis=0)).astype(BF16)
-    kv_ref[0:GROUP, 0:HEAD_L] = dot(pick, jnp.concatenate(keys, axis=0)).astype(BF16)
-    value = dot(pick, jnp.concatenate(values, axis=0))
+    packed = dot(pick, made)
+    q_ref[...] = packed[:, 0:HEAD_L].astype(BF16)
+    kv_ref[0:GROUP, 0:HEAD_L] = packed[:, HEAD_L : 2 * HEAD_L].astype(BF16)
+    value = packed[:, 2 * HEAD_L :]
     largest = jnp.max(jnp.max(jnp.abs(value), axis=1, keepdims=True), axis=0, keepdims=True)
     power = jnp.clip(13.0 - jnp.ceil(jnp.log2(jnp.maximum(largest, 1e-35))), -20.0, 100.0)
     kv_ref[0:GROUP, HEAD_L:] = (value * jnp.exp2(power)).astype(BF16)
@@ -131,7 +133,7 @@
 SCALE = 1.0 / (math.sqrt(HEAD_L) * math.log(2.0))
 
 
-def attend_kernel(z_ref, q_ref, kv_ref, out_ref, m_ref, l_ref, acc_ref):
+def attend_kernel(z_ref, q_ref, kv_ref, place_ref, w_ref, out_ref, theirs_ref, m_ref, l_ref, acc_ref):
     m_ref[...] = jnp.full(m_ref.shape, NEGATIVE, F32)
     l_ref[...] = jnp.zeros(l_ref.shape, F32)
     acc_ref[...] = jnp.zeros(acc_ref.shape, F32)
@@ -164,34 +166,38 @@
                 mixed = mixed + dot(weights[:, GROUP * k : GROUP * (k + 1)], kv_ref[b, 0:GROUP, HEAD_L:]) * back
             acc_ref[...] = mixed
 
-    out_ref[...] = (acc_ref[...] / l_ref[...]).astype(BF16)
-
-
-def share_kernel(mixed_ref, place_ref, w_ref, own_ref, other_ref):
-    slots = place_ref.shape[1]
-    blocks = slots // (2 * ROWS)
-    pick = (iota((GROUP, slots), 0) == place_ref[0:1]).astype(F32).astype(BF16)
-    spread = dot_tn(pick, mixed_ref[...]).astype(BF16)
-    width = own_ref.shape[2]
+    mixed = (acc_ref[...] / l_ref[...]).astype(BF16)
+    out_ref[...] = mixed
+    write_shares(mixed, place_ref, w_ref, theirs_ref, 1)
+
+
+def write_shares(mixed, place_ref, w_ref, shares_ref, half):
+    slots = place_ref.shape[1] // 2
+    place = place_ref[0:1][:, slots * half : slots * (half + 1)]
+    pick = (iota((GROUP, slots), 0) == place).astype(F32).astype(BF16)
+    spread = dot_tn(pick, mixed).astype(BF16)
+    width = shares_ref.shape[2]
     for t in range(4):
         part = dot(spread, w_ref[:, width * t : width * (t + 1)]).astype(BF16)
-        for c in range(2 * blocks):
-            dest_ref = own_ref if c < blocks else other_ref
-            dest_ref[4 * (c % blocks) + t] = part[ROWS * c : ROWS * c + SLOTS]
+        for c in range(slots // ROWS):
+            shares_ref[4 * c + t] = part[ROWS * c : ROWS * (c + 1)]
+
+
+def share_kernel(mixed_ref, place_ref, w_ref, mine_ref):
+    write_shares(mixed_ref[...], place_ref, w_ref, mine_ref, 0)
 
 
 def output_kernel(got_ref, enc_ref, member_ref, out_ref):
     decoded = got_ref[0].astype(F32)
     for h in range(1, got_ref.shape[0]):
         decoded = decoded + got_ref[h].astype(F32)
-    decoded = jnp.concatenate([decoded, jnp.zeros((ROWS - SLOTS, decoded.shape[1]), F32)], axis=0)
     high = decoded.astype(BF16)
     low = (decoded - high.astype(F32)).astype(BF16)
     members = member_ref[...]
     out_ref[...] = (enc_ref[...].astype(F32) + dot_tn(members, high) + dot_tn(members, low)).astype(BF16)
 
 
-def call(kernel, shapes, specs, *args, scratch=()):
+def call(kernel, shapes, specs, *args, scratch=(), grant=16):
     single = not isinstance(shapes, list)
     structs = [jax.ShapeDtypeStruct(s, d) for s, d in ([shapes] if single else shapes)]
     return pl.pallas_call(
@@ -200,6 +206,7 @@
         in_specs=specs,
         out_specs=VMEM if single else [VMEM] * len(structs),
         scratch_shapes=scratch,
+        compiler_params=pltpu.CompilerParams(vmem_limit_bytes=grant << 20),
     )(*args)
 
 
@@ -242,15 +249,15 @@
         [SMEM] + [VMEM] * 5,
         scalar(lax.axis_index("core")), own, other, latent_query, latent_key, latent_value,
     )
-    mixed = call(
+    shape = ((plane, SLOTS, width), BF16)
+    mixed, theirs = call(
         attend_kernel,
-        ((GROUP, HEAD_L), BF16),
-        [SMEM] + [VMEM] * 2,
-        scalar(lax.axis_index("bytes")), queries, gather_keys(kv),
-        scratch=[pltpu.VMEM((GROUP, HEAD_L), F32)] * 3,
-    )
-    shape = ((plane, SLOTS, width), BF16)
-    mine, theirs = call(share_kernel, [shape, shape], [VMEM] * 3, mixed, place, decode_weight)
+        [((GROUP, HEAD_L), BF16), shape],
+        [SMEM] + [VMEM] * 4,
+        scalar(lax.axis_index("bytes")), queries, gather_keys(kv), place, decode_weight,
+        scratch=[pltpu.VMEM((GROUP, HEAD_L), F32)] * 3, grant=32,
+    )
+    mine = call(share_kernel, shape, [VMEM] * 3, mixed, place, decode_weight)
     shares = (mine.astype(F32) + swap_cores(theirs).astype(F32)).astype(BF16)
     return call(output_kernel, ((n, width), BF16), [VMEM] * 3, exchange(shares), encoded, members)
 

time: 133 us -> 119 us (0.89)
  Pallas kernels: 19.4 us -> 7.63 us
  other arithmetic: 4.51 us -> 0.86 us
  local copies, waits for them, and re-layouts: 1.41 us -> 4.47 us
  waiting for transfers between devices: 5.06 us -> 2.7 us
    pallas_call x6, Pallas kernels: 19.4 us -> 7.63 us  [call(): pl.pallas_call(kernel, out_shape=structs[0] if single else structs, in_sp...]
    unnamed x6 -> x20, local copies, waits for them, and re-layouts: 1.41 us -> 4.47 us
    convert_element_type x1, other arithmetic: 2.33 us -> 0.67 us  [gather_keys(): return got.astype(BF16).reshape(size, *kv.shape)]
    ppermute x1, waiting for transfers between devices: 1.54 us -> 0.01 us  [per_device(): lax.ppermute(ids, ring, [(i, i + 1) for i in range(lax.axis_size(ring) -...]
    all_to_all x2, blocking collectives: 32.4 us -> 33.8 us  [exchange(): lax.all_to_all(value, ('x', 'tp'), split_axis=0, concat_axis=0, tiled=True)]
  transfers between devices with their start and end apart: 3 -> 3, of which waited for: 3 -> 2; matrix products, arithmetic and copies ran while one was open for 0% -> 0% of each run, Pallas kernels for 2% -> 1%
where the time goes in v1:
time: 119 us; the launch traced here: 118 us
  blocking collectives  86 us (72%)
  starting transfers between devices  16.7 us (14%)
  Pallas kernels  7.63 us (6%)
  local copies, waits for them, and re-layouts  4.47 us (4%)
  waiting for transfers between devices  2.7 us (2%)
    all_gather x1, blocking collectives, gather_keys(): got = lax.all_gather(kv.astype(jnp.float16), 'bytes', axis=0, tiled=True)  52.2 us
    all_to_all x2, blocking collectives, exchange(): lax.all_to_all(value, ('x', 'tp'), split_axis=0, concat_axis=0, tiled=True)  33.8 us
    ppermute x2, starting transfers between devices, swap_cores(): return lax.ppermute(value, 'core', [(0, 1), (1, 0)])  12.2 us
    pallas_call x6, Pallas kernels, call(): pl.pallas_call(kernel, out_shape=structs[0] if single else structs, in_sp...  7.63 us
    ppermute x1, starting transfers between devices, per_device(): lax.ppermute(ids, ring, [(i, i + 1) for i in range(lax.axis_size(ring) -...  4.49 us
    unnamed x20, local copies, waits for them, and re-layouts  4.47 us
    ppermute x2, waiting for transfers between devices, swap_cores(): return lax.ppermute(value, 'core', [(0, 1), (1, 0)])  2.7 us
  transfers between devices with their start and end apart: 3, of which 2 were waited for; matrix products, arithmetic and copies ran while one was open for 0% of the time, Pallas kernels for 1%

profile of v1, /device:TPU:1, one launch (start us, length us, event | category | flops | bytes accessed | tf_op | source)
XLA Modules:
  0.0 118.5 jit_solution(13528091957964414746)
XLA Ops:
  0.0 4.5 %collective-permute-start = (s32[192]{0:T(256)}, s32[192]{0:T(256)S(1)}, u32[]{:S(2)}, u32[]{:S(2)}) collective-permute-start(s32[192]{0:T(256)} %param.10), channel_id=1, source_target_pairs={{0,4},{4,8},{8,12},{12,16},{16,20},{20,24},{24,28},{28,32},{32,36}... | collective-permute-start | bytes 2312 | tf_op jit(solution)/shard_map/ppermute | solution.py:236
  4.5 0.0 copy-start.1
  4.5 1.0 copy-done.1
  5.5 0.0 copy-start.2
  5.5 1.0 copy-done.2
  6.6 1.0 copy-done.3
  7.6 1.0 copy-done.4
  8.7 0.7 shard_map.100.table_ref
  9.3 0.0 copy-start.5
  9.4 0.0 copy-start.6
  9.4 0.0 copy-start.7
  9.4 0.0 collective-permute-done
  9.4 0.0 copy-done.8
  9.4 0.0 copy-done.9
  9.4 1.7 %shard_map.101 = (bf16[192,256]{1,0:T(8,128)(2,1)S(1)}, bf16[72,192]{1,0:T(8,128)(2,1)S(1)}, bf16[16,72,256]{2,1,0:T(8,128)(2,1)S(1)}) custom-call(s32[1]{0:T(128)} %bitcast.2.block_ref, s32[1,192]{1,0:T(1,128)S(1)} %bitcast.8, s32[1,192]{1,0:T(1,128)S(1)} %bitcast.10, s32[1,192]{1,0:T(1,128)S(1)} %bitcast.9, bf16[256,768]{1,0:T(8,128)(2,1)S(1)} %shard_map.100.table_ref), custom_call_target="tpu_custom_call" | custom-call | tf_op jit(solution)/shard_map/pallas_call | solution.py:203
  11.1 19.3 %all_to_all.10.own_ref = bf16[16,72,256]{2,1,0:T(8,128)(2,1)S(1)} all-to-all(bf16[16,72,256]{2,1,0:T(8,128)(2,1)S(1)} %get-tuple-element.13), channel_id=1, replica_groups=mesh['bytes'=16,'x'=4,'core'=2,'tp'=4] {'x','tp'}, dimensions={0} | all-to-all | bytes 1179648 | tf_op jit(solution)/shard_map/all_to_all | solution.py:222
  30.4 2.3 %collective-permute-start.1 = (bf16[16,72,256]{2,1,0:T(8,128)(2,1)S(1)}, bf16[16,72,256]{2,1,0:T(8,128)(2,1)S(1)}, u32[]{:S(2)}, u32[]{:S(2)}) collective-permute-start(bf16[16,72,256]{2,1,0:T(8,128)(2,1)S(1)} %all_to_all.10.own_ref), channel_id=1, source_target_pairs={{0,4},{4,0},{1,5},{5,1},{2,6},{6,2},{3,7},{7,3},{8,12},{12,8},{9,1... | collective-permute-start | bytes 1769480 | tf_op jit(solution)/shard_map/ppermute | solution.py:218
  32.7 1.6 %collective-permute-done.1.other_ref = bf16[16,72,256]{2,1,0:T(8,128)(2,1)S(1)} collective-permute-done((bf16[16,72,256]{2,1,0:T(8,128)(2,1)S(1)}, bf16[16,72,256]{2,1,0:T(8,128)(2,1)S(1)}, u32[]{:S(2)}, u32[]{:S(2)}) %collective-permute-start.1) | collective-permute-done | bytes 589856 | tf_op jit(solution)/shard_map/ppermute | solution.py:218
  34.3 0.0 copy-done.5
  34.3 0.0 copy-done.6
  34.3 0.0 copy-done.7
  34.3 1.7 %shard_map.102 = (bf16[384,128]{1,0:T(8,128)(2,1)S(1)}, bf16[392,256]{1,0:T(8,128)(2,1)S(1)}, s32[8,576]{1,0:T(8,128)S(1)}) custom-call(s32[1]{0:T(128)} %bitcast.1.core_ref, bf16[16,72,256]{2,1,0:T(8,128)(2,1)S(1)} %all_to_all.10.own_ref, bf16[16,72,256]{2,1,0:T(8,128)(2,1)S(1)} %collective-permute-done.1.other_ref, bf16[1024,128]{1,0:T(8,128)(2,1)S(1)} %copy-done.5, ...), custom_call_target="tpu_custom_call" | custom-call | tf_op jit(solution)/shard_map/pallas_call | solution.py:203
  36.1 52.2 %all-gather.1 = f16[6272,256]{1,0:T(8,128)(2,1)S(1)} all-gather(f16[392,256]{1,0:T(8,128)(2,1)S(1)} %convert_element_type.15), channel_id=1, replica_groups=mesh['bytes'=16,'x'=4,'core'=2,'tp'=4] {'bytes'}, dimensions={0}, use_global_device_ids=true | all-gather | bytes 3411968 | tf_op jit(solution)/shard_map/all_gather | solution.py:227
  88.4 0.7 convert_element_type.16
  89.0 0.3 copy-done
  89.3 2.1 %shard_map.103 = (bf16[384,128]{1,0:T(8,128)(2,1)S(1)}, bf16[16,72,256]{2,1,0:T(8,128)(2,1)S(1)}) custom-call(s32[1]{0:T(128)} %bitcast.z_ref, bf16[384,128]{1,0:T(8,128)(2,1)S(1)} %get-tuple-element.14.q_ref, bf16[16,392,256]{2,1,0:T(8,128)(2,1)S(1)} %bitcast.7, s32[8,576]{1,0:T(8,128)S(1)} %get-tuple-element.16.place_ref, bf16[128,1024]{1,0:T(8,128)(2,1)S(1)} %copy-done), custom_call_target="tpu_custom_call" | custom-call | tf_op jit(solution)/shard_map/pallas_call | solution.py:203
  91.5 9.8 %collective-permute-start.2 = (bf16[16,72,256]{2,1,0:T(8,128)(2,1)S(1)}, bf16[16,72,256]{2,1,0:T(8,128)(2,1)S(1)}, u32[]{:S(2)}, u32[]{:S(2)}) collective-permute-start(bf16[16,72,256]{2,1,0:T(8,128)(2,1)S(1)} %get-tuple-element.18), channel_id=1, source_target_pairs={{0,4},{4,0},{1,5},{5,1},{2,6},{6,2},{3,7},{7,3},{8,12},{12,8},{9,1... | collective-permute-start | bytes 1769480 | tf_op jit(solution)/shard_map/ppermute | solution.py:218
  101.3 0.5 shard_map.104
  101.8 1.1 collective-permute-done.2
  102.9 0.2 add_convert_fusion
  103.1 14.5 %all_to_all.11.got_ref = bf16[16,72,256]{2,1,0:T(8,128)(2,1)S(1)} all-to-all(bf16[16,72,256]{2,1,0:T(8,128)(2,1)S(1)} %add_convert_fusion), channel_id=1, replica_groups=mesh['bytes'=16,'x'=4,'core'=2,'tp'=4] {'x','tp'}, dimensions={0} | all-to-all | bytes 1179648 | tf_op jit(solution)/shard_map/all_to_all | solution.py:222
  117.6 0.9 shard_map.105
  (6 shorter events, 0.0 us)
Async XLA Ops:
  0.0 9.4 %collective-permute-start = (s32[192]{0:T(256)}, s32[192]{0:T(256)S(1)}, u32[]{:S(2)}, u32[]{:S(2)}) collective-permute-start(s32[192]{0:T(256)} %param.10), channel_id=1, source_target_pairs={{0,4},{4,8},{8,12},{12,16},{16,20},{20,24},{24,28},{28,32},{32,36}... | collective-permute-start | bytes 2312 | tf_op jit(solution)/shard_map/ppermute | solution.py:236
  4.5 1.0 copy-start.1
  5.5 1.0 copy-start.2
  6.6 1.0 copy-start.3
  7.6 1.0 copy-start.4
  8.7 0.7 copy-start.8
  8.7 0.7 copy-start.9
  9.3 25.0 %copy-start.5 = (bf16[1024,128]{1,0:T(8,128)(2,1)S(1)}, bf16[1024,128]{1,0:T(8,128)(2,1)}, u32[]{:S(2)}) copy-start(bf16[1024,128]{1,0:T(8,128)(2,1)} %wq_ref.3) | copy-start | bytes 786436
  9.4 25.0 %copy-start.6 = (bf16[1024,128]{1,0:T(8,128)(2,1)S(1)}, bf16[1024,128]{1,0:T(8,128)(2,1)}, u32[]{:S(2)}) copy-start(bf16[1024,128]{1,0:T(8,128)(2,1)} %wk_ref.3) | copy-start | bytes 786436
  9.4 25.0 %copy-start.7 = (bf16[1024,128]{1,0:T(8,128)(2,1)S(1)}, bf16[1024,128]{1,0:T(8,128)(2,1)}, u32[]{:S(2)}) copy-start(bf16[1024,128]{1,0:T(8,128)(2,1)} %wv_ref.3) | copy-start | bytes 786436
  30.4 4.0 %collective-permute-start.1 = (bf16[16,72,256]{2,1,0:T(8,128)(2,1)S(1)}, bf16[16,72,256]{2,1,0:T(8,128)(2,1)S(1)}, u32[]{:S(2)}, u32[]{:S(2)}) collective-permute-start(bf16[16,72,256]{2,1,0:T(8,128)(2,1)S(1)} %all_to_all.10.own_ref), channel_id=1, source_target_pairs={{0,4},{4,0},{1,5},{5,1},{2,6},{6,2},{3,7},{7,3},{8,12},{12,8},{9,1... | collective-permute-start | bytes 1769480 | tf_op jit(solution)/shard_map/ppermute | solution.py:218
  88.4 1.0 copy-start
  91.5 11.4 %collective-permute-start.2 = (bf16[16,72,256]{2,1,0:T(8,128)(2,1)S(1)}, bf16[16,72,256]{2,1,0:T(8,128)(2,1)S(1)}, u32[]{:S(2)}, u32[]{:S(2)}) collective-permute-start(bf16[16,72,256]{2,1,0:T(8,128)(2,1)S(1)} %get-tuple-element.18), channel_id=1, source_target_pairs={{0,4},{4,0},{1,5},{5,1},{2,6},{6,2},{3,7},{7,3},{8,12},{12,8},{9,1... | collective-permute-start | bytes 1769480 | tf_op jit(solution)/shard_map/ppermute | solution.py:218

commit v2 on v1

--- a/solution.py
+++ b/solution.py
@@ -41,12 +41,28 @@
     return lax.dot_general(a, b, (((0,), (0,)), ((), ())), preferred_element_type=F32)
 
 
-def table_kernel(table_ref, wq_ref, wk_ref, wv_ref, out_ref):
+PIECES = 4
+
+
+def table_kernel(table_hbm, wq_hbm, wk_hbm, wv_hbm, out_ref, table_ref, wq_ref, wk_ref, wv_ref, sems):
+    pairs = ((table_hbm, table_ref), (wq_hbm, wq_ref), (wk_hbm, wk_ref), (wv_hbm, wv_ref))
+    copies = []
+    for k, (source, target) in enumerate(pairs):
+        rows = source.shape[0] // PIECES
+        part = [pl.ds(rows * i, rows) for i in range(PIECES)]
+        copies.append([pltpu.make_async_copy(source.at[p], target.at[p], sems.at[k, i]) for i, p in enumerate(part)])
+        for copy in copies[-1]:
+            copy.start()
+    for copy in copies[0]:
+        copy.wait()
     embedded = table_ref[...].astype(F32)
     scale = lax.rsqrt(jnp.mean(embedded * embedded, axis=-1, keepdims=True) + EPSILON)
     normed = (embedded * scale).astype(BF16)
+    width = wq_ref.shape[1]
     for k, w_ref in enumerate((wq_ref, wk_ref, wv_ref)):
-        out_ref[:, 256 * k : 256 * (k + 1)] = dot(normed, w_ref[...]).astype(BF16)
+        for copy in copies[k + 1]:
+            copy.wait()
+        out_ref[:, width * k : width * (k + 1)] = dot(normed, w_ref[...]).astype(BF16)
 
 
 def byte_kernel(block_ref, ids_ref, earlier_ref, offsets_ref, table_ref, enc_ref, member_ref, pay_ref):
@@ -90,21 +106,33 @@
         pay_ref[i] = payload
 
 
-def latent_kernel(core_ref, own_ref, other_ref, wq_ref, wk_ref, wv_ref, q_ref, kv_ref, place_ref):
-    blocks = own_ref.shape[0] // 4
+def project_blocks(got_ref, wq_ref, wk_ref, wv_ref):
+    weight = jnp.concatenate([wq_ref[...], wk_ref[...], wv_ref[...]], axis=1)
+    here, rows = [], []
+    for k in range(got_ref.shape[0] // 4):
+        parts = [got_ref[4 * k + t].astype(F32) for t in range(4)]
+        used = (parts[0][:, 0:1] < 0.1 * UNUSED).astype(F32)
+        here.append(jnp.sum(used, axis=0, keepdims=True))
+        square = sum(jnp.sum(p * p, axis=-1, keepdims=True) for p in parts)
+        scale = used * lax.rsqrt(square * (1.0 / DB) + EPSILON)
+        rows.append(jnp.concatenate([(p * scale).astype(BF16) for p in parts], axis=1))
+    return here, dot(jnp.concatenate(rows, axis=0), weight).astype(BF16)
+
+
+def own_latent_kernel(own_ref, wq_ref, wk_ref, wv_ref, made_ref, count_ref):
+    here, made = project_blocks(own_ref, wq_ref, wk_ref, wv_ref)
+    made_ref[...] = made
+    for k, filled in enumerate(here):
+        count_ref[k : k + 1] = jnp.broadcast_to(filled, (1, count_ref.shape[1]))
+
+
+def latent_kernel(core_ref, made_ref, count_ref, other_ref, wq_ref, wk_ref, wv_ref, q_ref, kv_ref, place_ref):
+    blocks = other_ref.shape[0] // 4
     slots = 2 * blocks * ROWS
     is_odd = (core_ref[0] > 0).astype(F32)
-    weight = jnp.concatenate([wq_ref[...], wk_ref[...], wv_ref[...]], axis=1)
-    here, rows = [], []
-    for r in (own_ref, other_ref):
-        for k in range(blocks):
-            parts = [r[4 * k + t].astype(F32) for t in range(4)]
-            used = (parts[0][:, 0:1] < 0.1 * UNUSED).astype(F32)
-            here.append(jnp.sum(used, axis=0, keepdims=True))
-            square = sum(jnp.sum(p * p, axis=-1, keepdims=True) for p in parts)
-            scale = used * lax.rsqrt(square * (1.0 / DB) + EPSILON)
-            rows.append(jnp.concatenate([(p * scale).astype(BF16) for p in parts], axis=1))
-    made = dot(jnp.concatenate(rows, axis=0), weight).astype(BF16)
+    here, made = project_blocks(other_ref, wq_ref, wk_ref, wv_ref)
+    here = [count_ref[k : k + 1, 0:1] for k in range(blocks)] + here
+    made = jnp.concatenate([made_ref[...], made], axis=0)
     slot = iota((1, slots), 1)
     place = jnp.full((1, slots), -1.0, F32)
     total = jnp.zeros((1, 1), F32)
@@ -234,7 +262,14 @@
     ring = ("bytes", "x", "core")
     plane = lax.axis_size(("x", "tp"))
     earlier = lax.ppermute(ids, ring, [(i, i + 1) for i in range(lax.axis_size(ring) - 1)])
-    table = call(table_kernel, ((byte_table.shape[0], 3 * width), BF16), [VMEM] * 4, byte_table, byte_query, byte_key, byte_value)
+    weights = [pltpu.with_memory_space_constraint(w, pltpu.HBM) for w in (byte_table, byte_query, byte_key, byte_value)]
+    table = call(
+        table_kernel,
+        ((byte_table.shape[0], 3 * width), BF16),
+        [pl.BlockSpec(memory_space=pltpu.HBM)] * 4,
+        *weights,
+        scratch=[pltpu.VMEM(w.shape, BF16) for w in weights] + [pltpu.SemaphoreType.DMA((4, PIECES))],
+    )
     encoded, members, payload = call(
         byte_kernel,
         [((n, width), BF16), ((ROWS, n), BF16), ((plane, ROWS, width), BF16)],
@@ -243,11 +278,16 @@
     )
     own = exchange(payload)
     other = swap_cores(own)
+    projections = (latent_query, latent_key, latent_value)
+    half = ROWS * plane // 4
+    made, counts = call(
+        own_latent_kernel, [((half, 3 * HEAD_L), BF16), ((8, HEAD_L), F32)], [VMEM] * 4, own, *projections
+    )
     queries, kv, place = call(
         latent_kernel,
-        [((GROUP, HEAD_L), BF16), ((KVROWS, 2 * HEAD_L), BF16), ((8, 2 * ROWS * plane // 4), jnp.int32)],
-        [SMEM] + [VMEM] * 5,
-        scalar(lax.axis_index("core")), own, other, latent_query, latent_key, latent_value,
+        [((GROUP, HEAD_L), BF16), ((KVROWS, 2 * HEAD_L), BF16), ((8, 2 * half), jnp.int32)],
+        [SMEM] + [VMEM] * 6,
+        scalar(lax.axis_index("core")), made, counts, other, *projections,
     )
     shape = ((plane, SLOTS, width), BF16)
     mixed, theirs = call(

time: 119 us -> 116 us (0.975)
  local copies, waits for them, and re-layouts: 4.47 us -> 0.31 us
  Pallas kernels: 7.63 us -> 9.82 us
  blocking collectives: 86 us -> 84.4 us
    unnamed x20 -> x12, local copies, waits for them, and re-layouts: 4.47 us -> 0.31 us
    pallas_call x6 -> x7, Pallas kernels: 7.63 us -> 9.82 us  [call(): pl.pallas_call(kernel, out_shape=structs[0] if single else structs, in_sp...]
    ppermute x1, waiting for transfers between devices: 0.01 us -> 1.8 us  [per_device(): lax.ppermute(ids, ring, [(i, i + 1) for i in range(lax.axis_size(ring) -...]
    all_to_all x2, blocking collectives: 33.8 us -> 32 us  [exchange(): lax.all_to_all(value, ('x', 'tp'), split_axis=0, concat_axis=0, tiled=True)]
  transfers between devices with their start and end apart: 3 -> 3, of which waited for: 2 -> 3; matrix products, arithmetic and copies ran while one was open for 0% -> 0% of each run, Pallas kernels for 1% -> 3%
where the time goes in v2:
time: 116 us; the launch traced here: 115 us
  blocking collectives  84.4 us (73%)
  starting transfers between devices  16 us (14%)
  Pallas kernels  9.82 us (8%)
  waiting for transfers between devices  3.7 us (3%)
    all_gather x1, blocking collectives, gather_keys(): got = lax.all_gather(kv.astype(jnp.float16), 'bytes', axis=0, tiled=True)  52.4 us
    all_to_all x2, blocking collectives, exchange(): lax.all_to_all(value, ('x', 'tp'), split_axis=0, concat_axis=0, tiled=True)  32 us
    ppermute x2, starting transfers between devices, swap_cores(): return lax.ppermute(value, 'core', [(0, 1), (1, 0)])  11.5 us
    pallas_call x7, Pallas kernels, call(): pl.pallas_call(kernel, out_shape=structs[0] if single else structs, in_sp...  9.82 us
    ppermute x1, starting transfers between devices, per_device(): lax.ppermute(ids, ring, [(i, i + 1) for i in range(lax.axis_size(ring) -...  4.49 us
  transfers between devices with their start and end apart: 3, of which 3 were waited for; matrix products, arithmetic and copies ran while one was open for 0% of the time, Pallas kernels for 3%

profile of v2, /device:TPU:1, one launch (start us, length us, event | category | flops | bytes accessed | tf_op | source)
XLA Modules:
  0.0 115.3 jit_solution(17574627340141700802)
XLA Ops:
  0.0 4.5 %collective-permute-start = (s32[192]{0:T(256)}, s32[192]{0:T(256)S(1)}, u32[]{:S(2)}, u32[]{:S(2)}) collective-permute-start(s32[192]{0:T(256)} %param.10), channel_id=1, source_target_pairs={{0,4},{4,8},{8,12},{12,16},{16,20},{20,24},{24,28},{28,32},{32,36}... | collective-permute-start | bytes 2312 | tf_op jit(solution)/shard_map/ppermute | solution.py:264
  4.5 0.0 copy-start.4
  4.5 0.0 copy-start.5
  4.5 2.6 %shard_map.100.table_ref = bf16[256,768]{1,0:T(8,128)(2,1)S(1)} custom-call(bf16[256,1024]{1,0:T(8,128)(2,1)} %table_hbm.1, bf16[1024,256]{1,0:T(8,128)(2,1)} %wq_hbm.1, bf16[1024,256]{1,0:T(8,128)(2,1)} %wk_hbm.1, bf16[1024,256]{1,0:T(8,128)(2,1)} %wv_hbm.1), custom_call_target="tpu_custom_call" | custom-call | tf_op jit(solution)/shard_map/pallas_call | solution.py:231
  7.1 0.0 copy-start.1
  7.1 0.0 copy-start.2
  7.2 0.0 copy-start.3
  7.2 1.8 %collective-permute-done = s32[192]{0:T(256)S(1)} collective-permute-done((s32[192]{0:T(256)}, s32[192]{0:T(256)S(1)}, u32[]{:S(2)}, u32[]{:S(2)}) %collective-permute-start) | collective-permute-done | bytes 800 | tf_op jit(solution)/shard_map/ppermute | solution.py:264
  9.0 0.0 copy-done.4
  9.0 0.0 copy-done.5
  9.0 1.7 %shard_map.101 = (bf16[192,256]{1,0:T(8,128)(2,1)S(1)}, bf16[72,192]{1,0:T(8,128)(2,1)S(1)}, bf16[16,72,256]{2,1,0:T(8,128)(2,1)S(1)}) custom-call(s32[1]{0:T(128)} %bitcast.2.block_ref, s32[1,192]{1,0:T(1,128)S(1)} %bitcast.8, s32[1,192]{1,0:T(1,128)S(1)} %bitcast.10, s32[1,192]{1,0:T(1,128)S(1)} %bitcast.9, bf16[256,768]{1,0:T(8,128)(2,1)S(1)} %shard_map.100.table_ref), custom_call_target="tpu_custom_call" | custom-call | tf_op jit(solution)/shard_map/pallas_call | solution.py:231
  10.6 17.5 %all_to_all.10.own_ref = bf16[16,72,256]{2,1,0:T(8,128)(2,1)S(1)} all-to-all(bf16[16,72,256]{2,1,0:T(8,128)(2,1)S(1)} %get-tuple-element.15), channel_id=1, replica_groups=mesh['bytes'=16,'x'=4,'core'=2,'tp'=4] {'x','tp'}, dimensions={0} | all-to-all | bytes 1179648 | tf_op jit(solution)/shard_map/all_to_all | solution.py:250
  28.1 2.4 %collective-permute-start.1 = (bf16[16,72,256]{2,1,0:T(8,128)(2,1)S(1)}, bf16[16,72,256]{2,1,0:T(8,128)(2,1)S(1)}, u32[]{:S(2)}, u32[]{:S(2)}) collective-permute-start(bf16[16,72,256]{2,1,0:T(8,128)(2,1)S(1)} %all_to_all.10.own_ref), channel_id=1, source_target_pairs={{0,4},{4,0},{1,5},{5,1},{2,6},{6,2},{3,7},{7,3},{8,12},{12,8},{9,1... | collective-permute-start | bytes 1769480 | tf_op jit(solution)/shard_map/ppermute | solution.py:246
  30.5 0.0 copy-done.1
  30.5 0.0 copy-done.2
  30.5 0.0 copy-done.3
  30.6 0.8 shard_map.102
  31.3 0.8 collective-permute-done.1.other_ref
  32.1 1.2 %shard_map.103 = (bf16[384,128]{1,0:T(8,128)(2,1)S(1)}, bf16[392,256]{1,0:T(8,128)(2,1)S(1)}, s32[8,576]{1,0:T(8,128)S(1)}) custom-call(s32[1]{0:T(128)} %bitcast.1.core_ref, bf16[288,384]{1,0:T(8,128)(2,1)S(1)} %get-tuple-element.16.made_ref, f32[8,128]{1,0:T(8,128)S(1)} %get-tuple-element.17.count_ref, ...), custom_call_target="tpu_custom_call" | custom-call | tf_op jit(solution)/shard_map/pallas_call | solution.py:231
  33.4 52.4 %all-gather.1 = f16[6272,256]{1,0:T(8,128)(2,1)S(1)} all-gather(f16[392,256]{1,0:T(8,128)(2,1)S(1)} %convert_element_type.15), channel_id=1, replica_groups=mesh['bytes'=16,'x'=4,'core'=2,'tp'=4] {'bytes'}, dimensions={0}, use_global_device_ids=true | all-gather | bytes 3411968 | tf_op jit(solution)/shard_map/all_gather | solution.py:255
  85.8 0.0 copy-start
  85.8 0.7 convert_element_type.16
  86.5 0.3 copy-done
  86.8 2.1 %shard_map.104 = (bf16[384,128]{1,0:T(8,128)(2,1)S(1)}, bf16[16,72,256]{2,1,0:T(8,128)(2,1)S(1)}) custom-call(s32[1]{0:T(128)} %bitcast.z_ref, bf16[384,128]{1,0:T(8,128)(2,1)S(1)} %get-tuple-element.18.q_ref, bf16[16,392,256]{2,1,0:T(8,128)(2,1)S(1)} %bitcast.7, s32[8,576]{1,0:T(8,128)S(1)} %get-tuple-element.20.place_ref, bf16[128,1024]{1,0:T(8,128)(2,1)S(1)} %copy-done), custom_call_target="tpu_custom_call" | custom-call | tf_op jit(solution)/shard_map/pallas_call | solution.py:231
  88.9 9.2 %collective-permute-start.2 = (bf16[16,72,256]{2,1,0:T(8,128)(2,1)S(1)}, bf16[16,72,256]{2,1,0:T(8,128)(2,1)S(1)}, u32[]{:S(2)}, u32[]{:S(2)}) collective-permute-start(bf16[16,72,256]{2,1,0:T(8,128)(2,1)S(1)} %get-tuple-element.22), channel_id=1, source_target_pairs={{0,4},{4,0},{1,5},{5,1},{2,6},{6,2},{3,7},{7,3},{8,12},{12,8},{9,1... | collective-permute-start | bytes 1769480 | tf_op jit(solution)/shard_map/ppermute | solution.py:246
  98.1 0.5 shard_map.105
  98.6 1.1 collective-permute-done.2
  99.7 0.2 add_convert_fusion
  99.9 14.5 %all_to_all.11.got_ref = bf16[16,72,256]{2,1,0:T(8,128)(2,1)S(1)} all-to-all(bf16[16,72,256]{2,1,0:T(8,128)(2,1)S(1)} %add_convert_fusion), channel_id=1, replica_groups=mesh['bytes'=16,'x'=4,'core'=2,'tp'=4] {'x','tp'}, dimensions={0} | all-to-all | bytes 1179648 | tf_op jit(solution)/shard_map/all_to_all | solution.py:250
  114.4 0.9 shard_map.106
  (1 shorter events, 0.0 us)
Async XLA Ops:
  0.0 9.0 %collective-permute-start = (s32[192]{0:T(256)}, s32[192]{0:T(256)S(1)}, u32[]{:S(2)}, u32[]{:S(2)}) collective-permute-start(s32[192]{0:T(256)} %param.10), channel_id=1, source_target_pairs={{0,4},{4,8},{8,12},{12,16},{16,20},{20,24},{24,28},{28,32},{32,36}... | collective-permute-start | bytes 2312 | tf_op jit(solution)/shard_map/ppermute | solution.py:264
  4.5 4.5 %copy-start.4 = (s32[192]{0:T(256)S(1)}, s32[192]{0:T(256)}, u32[]{:S(2)}) copy-start(s32[192]{0:T(256)} %param.10) | copy-start | bytes 2308
  4.5 4.5 %copy-start.5 = (s32[192]{0:T(256)S(1)}, s32[192]{0:T(256)}, u32[]{:S(2)}) copy-start(s32[192]{0:T(256)} %param.11) | copy-start | bytes 2308
  7.1 23.4 %copy-start.1 = (bf16[1024,128]{1,0:T(8,128)(2,1)S(1)}, bf16[1024,128]{1,0:T(8,128)(2,1)}, u32[]{:S(2)}) copy-start(bf16[1024,128]{1,0:T(8,128)(2,1)} %wq_ref.3) | copy-start | bytes 786436
  7.1 23.4 %copy-start.2 = (bf16[1024,128]{1,0:T(8,128)(2,1)S(1)}, bf16[1024,128]{1,0:T(8,128)(2,1)}, u32[]{:S(2)}) copy-start(bf16[1024,128]{1,0:T(8,128)(2,1)} %wk_ref.3) | copy-start | bytes 786436
  7.2 23.4 %copy-start.3 = (bf16[1024,128]{1,0:T(8,128)(2,1)S(1)}, bf16[1024,128]{1,0:T(8,128)(2,1)}, u32[]{:S(2)}) copy-start(bf16[1024,128]{1,0:T(8,128)(2,1)} %wv_ref.3) | copy-start | bytes 786436
  28.1 4.0 %collective-permute-start.1 = (bf16[16,72,256]{2,1,0:T(8,128)(2,1)S(1)}, bf16[16,72,256]{2,1,0:T(8,128)(2,1)S(1)}, u32[]{:S(2)}, u32[]{:S(2)}) collective-permute-start(bf16[16,72,256]{2,1,0:T(8,128)(2,1)S(1)} %all_to_all.10.own_ref), channel_id=1, source_target_pairs={{0,4},{4,0},{1,5},{5,1},{2,6},{6,2},{3,7},{7,3},{8,12},{12,8},{9,1... | collective-permute-start | bytes 1769480 | tf_op jit(solution)/shard_map/ppermute | solution.py:246
  85.8 1.0 copy-start
  88.9 10.8 %collective-permute-start.2 = (bf16[16,72,256]{2,1,0:T(8,128)(2,1)S(1)}, bf16[16,72,256]{2,1,0:T(8,128)(2,1)S(1)}, u32[]{:S(2)}, u32[]{:S(2)}) collective-permute-start(bf16[16,72,256]{2,1,0:T(8,128)(2,1)S(1)} %get-tuple-element.22), channel_id=1, source_target_pairs={{0,4},{4,0},{1,5},{5,1},{2,6},{6,2},{3,7},{7,3},{8,12},{12,8},{9,1... | collective-permute-start | bytes 1769480 | tf_op jit(solution)/shard_map/ppermute | solution.py:246

commit v3 on v2

--- a/solution.py
+++ b/solution.py
@@ -15,7 +15,7 @@
 UNUSED = 1e9
 GROUP = 384
 KVROWS = 392
-SPAN = 4
+SPANS = (1, 3, 4, 4, 4)
 EPSILON = 1e-06
 NEGATIVE = -1e30
 F32 = jnp.float32
@@ -65,41 +65,77 @@
         out_ref[:, width * k : width * (k + 1)] = dot(normed, w_ref[...]).astype(BF16)
 
 
-def byte_kernel(block_ref, ids_ref, earlier_ref, offsets_ref, table_ref, enc_ref, member_ref, pay_ref):
+HEAD_B = 64
+
+
+def head_column(width, h):
+    column = iota((1, width), 1)
+    return ((column >= h * HEAD_B) & (column < (h + 1) * HEAD_B)).astype(F32).astype(BF16)
+
+
+def spread_heads(columns, width):
+    which = iota((1, width), 1) // HEAD_B
+    out = jnp.broadcast_to(columns[0], (columns[0].shape[0], width))
+    for h in range(1, len(columns)):
+        out = jnp.where(which == h, columns[h], out)
+    return out
+
+
+def own_byte_kernel(ids_ref, offsets_ref, table_ref, q_ref, acc_ref, stat_ref, member_ref):
     n = ids_ref.shape[1]
-    vocab = table_ref.shape[0]
-    width = enc_ref.shape[1]
-    onehot = (iota((vocab, n), 0) == ids_ref[...]).astype(F32).astype(BF16)
-    onehot_e = (iota((vocab, n), 0) == earlier_ref[...]).astype(F32).astype(BF16)
+    width = q_ref.shape[1]
+    onehot = (iota((table_ref.shape[0], n), 0) == ids_ref[...]).astype(F32).astype(BF16)
     own = dot_tn(onehot, table_ref[...]).astype(BF16)
-    before = dot_tn(onehot_e, table_ref[:, width:]).astype(BF16)
-    queries = own[:, :width]
-    keys = jnp.concatenate([before[:, :width], own[:, width : 2 * width]], axis=0)
-    values = jnp.concatenate([before[:, width:], own[:, 2 * width :]], axis=0)
-    query_pos = iota((n, 2 * n), 0)
-    key_pos = iota((n, 2 * n), 1)
-    first = jnp.where(block_ref[0] > 0, 0, n)
-    allowed = (key_pos > query_pos) & (key_pos <= query_pos + n) & (key_pos >= first)
-    head = 64
-    encoded = jnp.zeros((n, width), F32)
-    for h in range(width // head):
-        column = iota((1, width), 1)
-        mine = ((column >= h * head) & (column < (h + 1) * head)).astype(F32).astype(BF16)
-        scores = dot_nt(queries * mine, keys) * (1.0 / math.sqrt(head))
-        scores = jnp.where(allowed, scores, NEGATIVE)
-        weights = jnp.exp(scores - jnp.max(scores, axis=-1, keepdims=True))
-        totals = jnp.sum(weights, axis=-1, keepdims=True)
-        encoded = encoded + dot(weights.astype(BF16), values * mine) / totals
-    encoded = encoded.astype(BF16)
-    enc_ref[...] = encoded
+    queries, keys, values = own[:, :width], own[:, width : 2 * width], own[:, 2 * width :]
+    q_ref[...] = queries
+    causal = iota((n, n), 1) <= iota((n, n), 0)
+    lane = iota((1, stat_ref.shape[1]), 1)
+    stats = jnp.zeros(stat_ref.shape, F32)
+    mixed = jnp.zeros((n, width), F32)
+    heads = width // HEAD_B
+    for h in range(heads):
+        mine = head_column(width, h)
+        scores = jnp.where(causal, dot_nt(queries * mine, keys) * (1.0 / math.sqrt(HEAD_B)), NEGATIVE)
+        highest = jnp.max(scores, axis=-1, keepdims=True)
+        weights = jnp.exp(scores - highest)
+        stats = jnp.where(lane == h, highest, stats)
+        stats = jnp.where(lane == heads + h, jnp.sum(weights, axis=-1, keepdims=True), stats)
+        mixed = mixed + dot(weights.astype(BF16), values * mine)
+    acc_ref[...] = mixed
+    stat_ref[...] = stats
     starts = (offsets_ref[...] == 0).astype(F32)
     upto = (iota((n, n), 0) <= iota((n, n), 1)).astype(F32).astype(BF16)
     running = dot(jnp.broadcast_to(starts, (8, n)).astype(BF16), upto)[0:1]
     patch = running.astype(jnp.int32) - 1
-    members = (iota((ROWS, n), 0) == patch).astype(F32)
-    member_ref[...] = members.astype(BF16)
-    lengths = jnp.sum(members, axis=1, keepdims=True)
-    pooled = dot(members.astype(BF16), encoded) / jnp.maximum(lengths, 1.0)
+    member_ref[...] = (iota((ROWS, n), 0) == patch).astype(F32).astype(BF16)
+
+
+def byte_kernel(block_ref, earlier_ref, table_ref, q_ref, acc_ref, stat_ref, member_ref, enc_ref, pay_ref):
+    n, width = q_ref.shape
+    onehot = (iota((table_ref.shape[0], n), 0) == earlier_ref[...]).astype(F32).astype(BF16)
+    before = dot_tn(onehot, table_ref[:, width:]).astype(BF16)
+    keys, values = before[:, :width], before[:, width:]
+    first = jnp.where(block_ref[0] > 0, 0, n)
+    allowed = (iota((n, n), 1) > iota((n, n), 0)) & (iota((n, n), 1) >= first)
+    queries = q_ref[...]
+    heads = width // HEAD_B
+    mixed = jnp.zeros((n, width), F32)
+    factors, totals = [], []
+    for h in range(heads):
+        mine = head_column(width, h)
+        scores = jnp.where(allowed, dot_nt(queries * mine, keys) * (1.0 / math.sqrt(HEAD_B)), NEGATIVE)
+        old = stat_ref[:, h : h + 1]
+        highest = jnp.maximum(old, jnp.max(scores, axis=-1, keepdims=True))
+        weights = jnp.exp(scores - highest)
+        factors.append(jnp.exp(old - highest))
+        totals.append(stat_ref[:, heads + h : heads + h + 1] * factors[-1] + jnp.sum(weights, axis=-1, keepdims=True))
+        mixed = mixed + dot(weights.astype(BF16), values * mine)
+    mixed = mixed + acc_ref[...] * spread_heads(factors, width)
+    encoded = (mixed / spread_heads(totals, width)).astype(BF16)
+    enc_ref[...] = encoded
+    members = member_ref[...]
+    lengths = jnp.sum(members.astype(F32), axis=1, keepdims=True)
+    pooled = dot(members, encoded) / jnp.maximum(lengths, 1.0)
     empty = (lengths < 0.5) & (iota((ROWS, width), 1) == 0)
     payload = jnp.where(empty, UNUSED, pooled).astype(BF16)
     for i in range(pay_ref.shape[0]):
@@ -161,17 +197,25 @@
 SCALE = 1.0 / (math.sqrt(HEAD_L) * math.log(2.0))
 
 
-def attend_kernel(z_ref, q_ref, kv_ref, place_ref, w_ref, out_ref, theirs_ref, m_ref, l_ref, acc_ref):
+def attend_kernel(z_ref, q_ref, kv_ref, place_ref, w_hbm, out_ref, theirs_ref, m_ref, l_ref, acc_ref, w_ref, sem):
+    load = pltpu.make_async_copy(w_hbm, w_ref, sem)
+    load.start()
     m_ref[...] = jnp.full(m_ref.shape, NEGATIVE, F32)
     l_ref[...] = jnp.zeros(l_ref.shape, F32)
     acc_ref[...] = jnp.zeros(acc_ref.shape, F32)
     z = z_ref[0]
-    for tile in range(kv_ref.shape[0] // SPAN):
-
-        @pl.when(z >= tile * SPAN)
-        def _(tile=tile):
+    count = kv_ref.shape[0]
+    spans, done = [], 0
+    for span in SPANS + (4,) * count:
+        if done < count:
+            spans.append((done, min(done + span, count)))
+            done += span
+    for begin, end in spans:
+
+        @pl.when(z >= begin)
+        def _(begin=begin, end=end):
             codes, scores = [], []
-            for b in range(tile * SPAN, (tile + 1) * SPAN):
+            for b in range(begin, end):
                 filled = kv_ref[b, GROUP : GROUP + 1, 0:1].astype(F32) + kv_ref[b, GROUP + 1 : GROUP + 2, 0:1].astype(F32)
                 spot = iota((1, GROUP), 1)
                 past = jnp.where(spot.astype(F32) < filled, -1, GROUP)
@@ -188,14 +232,14 @@
             l_ref[...] = l_ref[...] * factor + jnp.sum(weights, axis=-1, keepdims=True)
             weights = weights.astype(BF16)
             mixed = acc_ref[...] * factor
-            for k in range(SPAN):
-                b = tile * SPAN + k
+            for k, b in enumerate(range(begin, end)):
                 back = jnp.exp2(-kv_ref[b, GROUP + 2 : GROUP + 3, 0:1].astype(F32))
                 mixed = mixed + dot(weights[:, GROUP * k : GROUP * (k + 1)], kv_ref[b, 0:GROUP, HEAD_L:]) * back
             acc_ref[...] = mixed
 
     mixed = (acc_ref[...] / l_ref[...]).astype(BF16)
     out_ref[...] = mixed
+    load.wait()
     write_shares(mixed, place_ref, w_ref, theirs_ref, 1)
 
 
@@ -270,11 +314,18 @@
         *weights,
         scratch=[pltpu.VMEM(w.shape, BF16) for w in weights] + [pltpu.SemaphoreType.DMA((4, PIECES))],
     )
-    encoded, members, payload = call(
+    part = call(
+        own_byte_kernel,
+        [((n, width), BF16), ((n, width), F32), ((n, HEAD_L), F32), ((ROWS, n), BF16)],
+        [VMEM] * 3,
+        ids.reshape(1, n), offsets.reshape(1, n), table,
+    )
+    members = part[3]
+    encoded, payload = call(
         byte_kernel,
-        [((n, width), BF16), ((ROWS, n), BF16), ((plane, ROWS, width), BF16)],
-        [SMEM] + [VMEM] * 4,
-        scalar(lax.axis_index(ring)), ids.reshape(1, n), earlier.reshape(1, n), offsets.reshape(1, n), table,
+        [((n, width), BF16), ((plane, ROWS, width), BF16)],
+        [SMEM] + [VMEM] * 6,
+        scalar(lax.axis_index(ring)), earlier.reshape(1, n), table, *part,
     )
     own = exchange(payload)
     other = swap_cores(own)
@@ -290,14 +341,17 @@
         scalar(lax.axis_index("core")), made, counts, other, *projections,
     )
     shape = ((plane, SLOTS, width), BF16)
+    decode = pltpu.with_memory_space_constraint(decode_weight, pltpu.HBM)
     mixed, theirs = call(
         attend_kernel,
         [((GROUP, HEAD_L), BF16), shape],
-        [SMEM] + [VMEM] * 4,
-        scalar(lax.axis_index("bytes")), queries, gather_keys(kv), place, decode_weight,
-        scratch=[pltpu.VMEM((GROUP, HEAD_L), F32)] * 3, grant=32,
-    )
-    mine = call(share_kernel, shape, [VMEM] * 3, mixed, place, decode_weight)
+        [SMEM] + [VMEM] * 3 + [pl.BlockSpec(memory_space=pltpu.HBM)],
+        scalar(lax.axis_index("bytes")), queries, gather_keys(kv), place, decode,
+        scratch=[pltpu.VMEM((GROUP, HEAD_L), F32)] * 3
+        + [pltpu.VMEM(decode_weight.shape, BF16), pltpu.SemaphoreType.DMA(())],
+        grant=32,
+    )
+    mine = call(share_kernel, shape, [VMEM] * 3, mixed, place, decode)
     shares = (mine.astype(F32) + swap_cores(theirs).astype(F32)).astype(BF16)
     return call(output_kernel, ((n, width), BF16), [VMEM] * 3, exchange(shares), encoded, members)
 

time: 116 us -> 117 us (level)
  Pallas kernels: 9.82 us -> 12.1 us
  waiting for transfers between devices: 3.7 us -> 1.93 us
    pallas_call x7 -> x8, Pallas kernels: 9.82 us -> 12.1 us  [call(): pl.pallas_call(kernel, out_shape=structs[0] if single else structs, in_sp...]
  transfers between devices with their start and end apart: 3 -> 3, of which waited for: 3 -> 3; matrix products, arithmetic and copies ran while one was open for 0% -> 0% of each run, Pallas kernels for 3% -> 5%
where the time goes in v3:
time: 117 us; the launch traced here: 116 us
  blocking collectives  85.3 us (73%)
  starting transfers between devices  15.8 us (14%)
  Pallas kernels  12.1 us (10%)
  waiting for transfers between devices  1.93 us (2%)
    all_gather x1, blocking collectives, gather_keys(): got = lax.all_gather(kv.astype(jnp.float16), 'bytes', axis=0, tiled=True)  52.4 us
    all_to_all x2, blocking collectives, exchange(): lax.all_to_all(value, ('x', 'tp'), split_axis=0, concat_axis=0, tiled=True)  32.9 us
    pallas_call x8, Pallas kernels, call(): pl.pallas_call(kernel, out_shape=structs[0] if single else structs, in_sp...  12.1 us
    ppermute x2, starting transfers between devices, swap_cores(): return lax.ppermute(value, 'core', [(0, 1), (1, 0)])  11.3 us
    ppermute x1, starting transfers between devices, per_device(): lax.ppermute(ids, ring, [(i, i + 1) for i in range(lax.axis_size(ring) -...  4.49 us
  transfers between devices with their start and end apart: 3, of which 3 were waited for; matrix products, arithmetic and copies ran while one was open for 0% of the time, Pallas kernels for 5%

profile of v3, /device:TPU:1, one launch (start us, length us, event | category | flops | bytes accessed | tf_op | source)
XLA Modules:
  0.0 116.2 jit_solution(2379286495648918189)
XLA Ops:
  0.0 4.5 %collective-permute-start = (s32[192]{0:T(256)}, s32[192]{0:T(256)S(1)}, u32[]{:S(2)}, u32[]{:S(2)}) collective-permute-start(s32[192]{0:T(256)} %param.10), channel_id=1, source_target_pairs={{0,4},{4,8},{8,12},{12,16},{16,20},{20,24},{24,28},{28,32},{32,36}... | collective-permute-start | bytes 2312 | tf_op jit(solution)/shard_map/ppermute | solution.py:308
  4.5 0.0 copy-start.3
  4.5 0.0 copy-start.4
  4.5 2.6 %shard_map.100.table_ref = bf16[256,768]{1,0:T(8,128)(2,1)S(1)} custom-call(bf16[256,1024]{1,0:T(8,128)(2,1)} %table_hbm.1, bf16[1024,256]{1,0:T(8,128)(2,1)} %wq_hbm.1, bf16[1024,256]{1,0:T(8,128)(2,1)} %wk_hbm.1, bf16[1024,256]{1,0:T(8,128)(2,1)} %wv_hbm.1), custom_call_target="tpu_custom_call" | custom-call | tf_op jit(solution)/shard_map/pallas_call | solution.py:275
  7.1 0.0 copy-done.3
  7.1 0.0 copy-done.4
  7.2 0.0 copy-start
  7.2 0.0 copy-start.1
  7.2 0.0 copy-start.2
  7.2 0.8 shard_map.101
  8.0 1.0 collective-permute-done
  9.0 2.7 %shard_map.102 = (bf16[192,256]{1,0:T(8,128)(2,1)S(1)}, bf16[16,72,256]{2,1,0:T(8,128)(2,1)S(1)}) custom-call(s32[1]{0:T(128)} %bitcast.2.block_ref, s32[1,192]{1,0:T(1,128)S(1)} %bitcast.10, bf16[256,768]{1,0:T(8,128)(2,1)S(1)} %shard_map.100.table_ref, bf16[192,256]{1,0:T(8,128)(2,1)S(1)} %get-tuple-element.18.q_ref, ...), custom_call_target="tpu_custom_call" | custom-call | tf_op jit(solution)/shard_map/pallas_call | solution.py:275
  11.7 18.3 %all_to_all.10.own_ref = bf16[16,72,256]{2,1,0:T(8,128)(2,1)S(1)} all-to-all(bf16[16,72,256]{2,1,0:T(8,128)(2,1)S(1)} %get-tuple-element.22), channel_id=1, replica_groups=mesh['bytes'=16,'x'=4,'core'=2,'tp'=4] {'x','tp'}, dimensions={0} | all-to-all | bytes 1179648 | tf_op jit(solution)/shard_map/all_to_all | solution.py:294
  30.0 2.3 %collective-permute-start.1 = (bf16[16,72,256]{2,1,0:T(8,128)(2,1)S(1)}, bf16[16,72,256]{2,1,0:T(8,128)(2,1)S(1)}, u32[]{:S(2)}, u32[]{:S(2)}) collective-permute-start(bf16[16,72,256]{2,1,0:T(8,128)(2,1)S(1)} %all_to_all.10.own_ref), channel_id=1, source_target_pairs={{0,4},{4,0},{1,5},{5,1},{2,6},{6,2},{3,7},{7,3},{8,12},{12,8},{9,1... | collective-permute-start | bytes 1769480 | tf_op jit(solution)/shard_map/ppermute | solution.py:290
  32.4 0.0 copy-done
  32.4 0.0 copy-done.1
  32.4 0.0 copy-done.2
  32.4 0.8 shard_map.103
  33.2 0.8 collective-permute-done.1.other_ref
  34.0 1.2 %shard_map.104 = (bf16[384,128]{1,0:T(8,128)(2,1)S(1)}, bf16[392,256]{1,0:T(8,128)(2,1)S(1)}, s32[8,576]{1,0:T(8,128)S(1)}) custom-call(s32[1]{0:T(128)} %bitcast.1.core_ref, bf16[288,384]{1,0:T(8,128)(2,1)S(1)} %get-tuple-element.23.made_ref, f32[8,128]{1,0:T(8,128)S(1)} %get-tuple-element.24.count_ref, ...), custom_call_target="tpu_custom_call" | custom-call | tf_op jit(solution)/shard_map/pallas_call | solution.py:275
  35.3 52.4 %all-gather.1 = f16[6272,256]{1,0:T(8,128)(2,1)S(1)} all-gather(f16[392,256]{1,0:T(8,128)(2,1)S(1)} %convert_element_type.15), channel_id=1, replica_groups=mesh['bytes'=16,'x'=4,'core'=2,'tp'=4] {'bytes'}, dimensions={0}, use_global_device_ids=true | all-gather | bytes 3411968 | tf_op jit(solution)/shard_map/all_gather | solution.py:299
  87.7 0.7 convert_element_type.16
  88.4 1.6 %shard_map.105 = (bf16[384,128]{1,0:T(8,128)(2,1)S(1)}, bf16[16,72,256]{2,1,0:T(8,128)(2,1)S(1)}) custom-call(s32[1]{0:T(128)} %bitcast.z_ref, bf16[384,128]{1,0:T(8,128)(2,1)S(1)} %get-tuple-element.25.q_ref, bf16[16,392,256]{2,1,0:T(8,128)(2,1)S(1)} %bitcast.7, s32[8,576]{1,0:T(8,128)S(1)} %get-tuple-element.27.place_ref, bf16[128,1024]{1,0:T(8,128)(2,1)} %w_ref.1), custom_call_target="tpu_custom_call" | custom-call | tf_op jit(solution)/shard_map/pallas_call | solution.py:275
  90.0 9.0 %collective-permute-start.2 = (bf16[16,72,256]{2,1,0:T(8,128)(2,1)S(1)}, bf16[16,72,256]{2,1,0:T(8,128)(2,1)S(1)}, u32[]{:S(2)}, u32[]{:S(2)}) collective-permute-start(bf16[16,72,256]{2,1,0:T(8,128)(2,1)S(1)} %get-tuple-element.29), channel_id=1, source_target_pairs={{0,4},{4,0},{1,5},{5,1},{2,6},{6,2},{3,7},{7,3},{8,12},{12,8},{9,1... | collective-permute-start | bytes 1769480 | tf_op jit(solution)/shard_map/ppermute | solution.py:290
  99.0 1.5 %shard_map.106 = bf16[16,72,256]{2,1,0:T(8,128)(2,1)S(1)} custom-call(bf16[384,128]{1,0:T(8,128)(2,1)S(1)} %get-tuple-element.28.mixed_ref, s32[8,576]{1,0:T(8,128)S(1)} %get-tuple-element.27.place_ref, bf16[128,1024]{1,0:T(8,128)(2,1)} %w_ref.1), custom_call_target="tpu_custom_call" | custom-call | tf_op jit(solution)/shard_map/pallas_call | solution.py:275
  100.4 0.1 collective-permute-done.2
  100.6 0.2 add_convert_fusion
  100.7 14.6 %all_to_all.11.got_ref = bf16[16,72,256]{2,1,0:T(8,128)(2,1)S(1)} all-to-all(bf16[16,72,256]{2,1,0:T(8,128)(2,1)S(1)} %add_convert_fusion), channel_id=1, replica_groups=mesh['bytes'=16,'x'=4,'core'=2,'tp'=4] {'x','tp'}, dimensions={0} | all-to-all | bytes 1179648 | tf_op jit(solution)/shard_map/all_to_all | solution.py:294
  115.3 0.9 shard_map.107
  (1 shorter events, 0.0 us)
Async XLA Ops:
  0.0 9.0 %collective-permute-start = (s32[192]{0:T(256)}, s32[192]{0:T(256)S(1)}, u32[]{:S(2)}, u32[]{:S(2)}) collective-permute-start(s32[192]{0:T(256)} %param.10), channel_id=1, source_target_pairs={{0,4},{4,8},{8,12},{12,16},{16,20},{20,24},{24,28},{28,32},{32,36}... | collective-permute-start | bytes 2312 | tf_op jit(solution)/shard_map/ppermute | solution.py:308
  4.5 2.6 %copy-start.3 = (s32[192]{0:T(256)S(1)}, s32[192]{0:T(256)}, u32[]{:S(2)}) copy-start(s32[192]{0:T(256)} %param.11) | copy-start | bytes 2308
  4.5 2.6 %copy-start.4 = (s32[192]{0:T(256)S(1)}, s32[192]{0:T(256)}, u32[]{:S(2)}) copy-start(s32[192]{0:T(256)} %param.10) | copy-start | bytes 2308
  7.2 25.2 %copy-start = (bf16[1024,128]{1,0:T(8,128)(2,1)S(1)}, bf16[1024,128]{1,0:T(8,128)(2,1)}, u32[]{:S(2)}) copy-start(bf16[1024,128]{1,0:T(8,128)(2,1)} %wq_ref.3) | copy-start | bytes 786436
  7.2 25.2 %copy-start.1 = (bf16[1024,128]{1,0:T(8,128)(2,1)S(1)}, bf16[1024,128]{1,0:T(8,128)(2,1)}, u32[]{:S(2)}) copy-start(bf16[1024,128]{1,0:T(8,128)(2,1)} %wk_ref.3) | copy-start | bytes 786436
  7.2 25.2 %copy-start.2 = (bf16[1024,128]{1,0:T(8,128)(2,1)S(1)}, bf16[1024,128]{1,0:T(8,128)(2,1)}, u32[]{:S(2)}) copy-start(bf16[1024,128]{1,0:T(8,128)(2,1)} %wv_ref.3) | copy-start | bytes 786436
  30.0 4.0 %collective-permute-start.1 = (bf16[16,72,256]{2,1,0:T(8,128)(2,1)S(1)}, bf16[16,72,256]{2,1,0:T(8,128)(2,1)S(1)}, u32[]{:S(2)}, u32[]{:S(2)}) collective-permute-start(bf16[16,72,256]{2,1,0:T(8,128)(2,1)S(1)} %all_to_all.10.own_ref), channel_id=1, source_target_pairs={{0,4},{4,0},{1,5},{5,1},{2,6},{6,2},{3,7},{7,3},{8,12},{12,8},{9,1... | collective-permute-start | bytes 1769480 | tf_op jit(solution)/shard_map/ppermute | solution.py:290
  90.0 10.6 %collective-permute-start.2 = (bf16[16,72,256]{2,1,0:T(8,128)(2,1)S(1)}, bf16[16,72,256]{2,1,0:T(8,128)(2,1)S(1)}, u32[]{:S(2)}, u32[]{:S(2)}) collective-permute-start(bf16[16,72,256]{2,1,0:T(8,128)(2,1)S(1)} %get-tuple-element.29), channel_id=1, source_target_pairs={{0,4},{4,0},{1,5},{5,1},{2,6},{6,2},{3,7},{7,3},{8,12},{12,8},{9,1... | collective-permute-start | bytes 1769480 | tf_op jit(solution)/shard_map/ppermute | solution.py:290

commit v4 on v3

--- a/solution.py
+++ b/solution.py
@@ -73,36 +73,10 @@
     return ((column >= h * HEAD_B) & (column < (h + 1) * HEAD_B)).astype(F32).astype(BF16)
 
 
-def spread_heads(columns, width):
-    which = iota((1, width), 1) // HEAD_B
-    out = jnp.broadcast_to(columns[0], (columns[0].shape[0], width))
-    for h in range(1, len(columns)):
-        out = jnp.where(which == h, columns[h], out)
-    return out
-
-
-def own_byte_kernel(ids_ref, offsets_ref, table_ref, q_ref, acc_ref, stat_ref, member_ref):
+def own_byte_kernel(ids_ref, offsets_ref, table_ref, own_ref, member_ref):
     n = ids_ref.shape[1]
-    width = q_ref.shape[1]
     onehot = (iota((table_ref.shape[0], n), 0) == ids_ref[...]).astype(F32).astype(BF16)
-    own = dot_tn(onehot, table_ref[...]).astype(BF16)
-    queries, keys, values = own[:, :width], own[:, width : 2 * width], own[:, 2 * width :]
-    q_ref[...] = queries
-    causal = iota((n, n), 1) <= iota((n, n), 0)
-    lane = iota((1, stat_ref.shape[1]), 1)
-    stats = jnp.zeros(stat_ref.shape, F32)
-    mixed = jnp.zeros((n, width), F32)
-    heads = width // HEAD_B
-    for h in range(heads):
-        mine = head_column(width, h)
-        scores = jnp.where(causal, dot_nt(queries * mine, keys) * (1.0 / math.sqrt(HEAD_B)), NEGATIVE)
-        highest = jnp.max(scores, axis=-1, keepdims=True)
-        weights = jnp.exp(scores - highest)
-        stats = jnp.where(lane == h, highest, stats)
-        stats = jnp.where(lane == heads + h, jnp.sum(weights, axis=-1, keepdims=True), stats)
-        mixed = mixed + dot(weights.astype(BF16), values * mine)
-    acc_ref[...] = mixed
-    stat_ref[...] = stats
+    own_ref[...] = dot_tn(onehot, table_ref[...]).astype(BF16)
     starts = (offsets_ref[...] == 0).astype(F32)
     upto = (iota((n, n), 0) <= iota((n, n), 1)).astype(F32).astype(BF16)
     running = dot(jnp.broadcast_to(starts, (8, n)).astype(BF16), upto)[0:1]
@@ -110,28 +84,27 @@
     member_ref[...] = (iota((ROWS, n), 0) == patch).astype(F32).astype(BF16)
 
 
-def byte_kernel(block_ref, earlier_ref, table_ref, q_ref, acc_ref, stat_ref, member_ref, enc_ref, pay_ref):
-    n, width = q_ref.shape
+def byte_kernel(block_ref, earlier_ref, table_ref, own_ref, member_ref, enc_ref, pay_ref):
+    n, width = enc_ref.shape
     onehot = (iota((table_ref.shape[0], n), 0) == earlier_ref[...]).astype(F32).astype(BF16)
     before = dot_tn(onehot, table_ref[:, width:]).astype(BF16)
-    keys, values = before[:, :width], before[:, width:]
+    own = own_ref[...]
+    queries = own[:, :width]
+    keys = jnp.concatenate([before[:, :width], own[:, width : 2 * width]], axis=0)
+    values = jnp.concatenate([before[:, width:], own[:, 2 * width :]], axis=0)
+    query_pos = iota((n, 2 * n), 0)
+    key_pos = iota((n, 2 * n), 1)
     first = jnp.where(block_ref[0] > 0, 0, n)
-    allowed = (iota((n, n), 1) > iota((n, n), 0)) & (iota((n, n), 1) >= first)
-    queries = q_ref[...]
-    heads = width // HEAD_B
-    mixed = jnp.zeros((n, width), F32)
-    factors, totals = [], []
-    for h in range(heads):
+    allowed = (key_pos > query_pos) & (key_pos <= query_pos + n) & (key_pos >= first)
+    encoded = jnp.zeros((n, width), F32)
+    for h in range(width // HEAD_B):
         mine = head_column(width, h)
-        scores = jnp.where(allowed, dot_nt(queries * mine, keys) * (1.0 / math.sqrt(HEAD_B)), NEGATIVE)
-        old = stat_ref[:, h : h + 1]
-        highest = jnp.maximum(old, jnp.max(scores, axis=-1, keepdims=True))
-        weights = jnp.exp(scores - highest)
-        factors.append(jnp.exp(old - highest))
-        totals.append(stat_ref[:, heads + h : heads + h + 1] * factors[-1] + jnp.sum(weights, axis=-1, keepdims=True))
-        mixed = mixed + dot(weights.astype(BF16), values * mine)
-    mixed = mixed + acc_ref[...] * spread_heads(factors, width)
-    encoded = (mixed / spread_heads(totals, width)).astype(BF16)
+        scores = dot_nt(queries * mine, keys) * (1.0 / math.sqrt(HEAD_B))
+        scores = jnp.where(allowed, scores, NEGATIVE)
+        weights = jnp.exp(scores - jnp.max(scores, axis=-1, keepdims=True))
+        totals = jnp.sum(weights, axis=-1, keepdims=True)
+        encoded = encoded + dot(weights.astype(BF16), values * mine) / totals
+    encoded = encoded.astype(BF16)
     enc_ref[...] = encoded
     members = member_ref[...]
     lengths = jnp.sum(members.astype(F32), axis=1, keepdims=True)
@@ -314,18 +287,17 @@
         *weights,
         scratch=[pltpu.VMEM(w.shape, BF16) for w in weights] + [pltpu.SemaphoreType.DMA((4, PIECES))],
     )
-    part = call(
+    looked_up, members = call(
         own_byte_kernel,
-        [((n, width), BF16), ((n, width), F32), ((n, HEAD_L), F32), ((ROWS, n), BF16)],
+        [((n, 3 * width), BF16), ((ROWS, n), BF16)],
         [VMEM] * 3,
         ids.reshape(1, n), offsets.reshape(1, n), table,
     )
-    members = part[3]
     encoded, payload = call(
         byte_kernel,
         [((n, width), BF16), ((plane, ROWS, width), BF16)],
-        [SMEM] + [VMEM] * 6,
-        scalar(lax.axis_index(ring)), earlier.reshape(1, n), table, *part,
+        [SMEM] + [VMEM] * 4,
+        scalar(lax.axis_index(ring)), earlier.reshape(1, n), table, looked_up, members,
     )
     own = exchange(payload)
     other = swap_cores(own)

time: 117 us -> 115 us (0.983)
  Pallas kernels: 12.1 us -> 10.2 us
    pallas_call x8, Pallas kernels: 12.1 us -> 10.2 us  [call(): pl.pallas_call(kernel, out_shape=structs[0] if single else structs, in_sp...]
  transfers between devices with their start and end apart: 3 -> 3, of which waited for: 3 -> 3; matrix products, arithmetic and copies ran while one was open for 0% -> 0% of each run, Pallas kernels for 5% -> 4%
where the time goes in v4:
time: 115 us; the launch traced here: 114 us
  blocking collectives  84.8 us (74%)
  starting transfers between devices  16 us (14%)
  Pallas kernels  10.2 us (9%)
  waiting for transfers between devices  2.44 us (2%)
    all_gather x1, blocking collectives, gather_keys(): got = lax.all_gather(kv.astype(jnp.float16), 'bytes', axis=0, tiled=True)  52.4 us
    all_to_all x2, blocking collectives, exchange(): lax.all_to_all(value, ('x', 'tp'), split_axis=0, concat_axis=0, tiled=True)  32.4 us
    ppermute x2, starting transfers between devices, swap_cores(): return lax.ppermute(value, 'core', [(0, 1), (1, 0)])  11.5 us
    pallas_call x8, Pallas kernels, call(): pl.pallas_call(kernel, out_shape=structs[0] if single else structs, in_sp...  10.2 us
    ppermute x1, starting transfers between devices, per_device(): lax.ppermute(ids, ring, [(i, i + 1) for i in range(lax.axis_size(ring) -...  4.49 us
  transfers between devices with their start and end apart: 3, of which 3 were waited for; matrix products, arithmetic and copies ran while one was open for 0% of the time, Pallas kernels for 4%

profile of v4, /device:TPU:1, one launch (start us, length us, event | category | flops | bytes accessed | tf_op | source)
XLA Modules:
  0.0 114.5 jit_solution(11625373726400999110)
XLA Ops:
  0.0 4.5 %collective-permute-start = (s32[192]{0:T(256)}, s32[192]{0:T(256)S(1)}, u32[]{:S(2)}, u32[]{:S(2)}) collective-permute-start(s32[192]{0:T(256)} %param.10), channel_id=1, source_target_pairs={{0,4},{4,8},{8,12},{12,16},{16,20},{20,24},{24,28},{28,32},{32,36}... | collective-permute-start | bytes 2312 | tf_op jit(solution)/shard_map/ppermute | solution.py:281
  4.5 0.0 copy-start.3
  4.5 0.0 copy-start.4
  4.5 2.6 %shard_map.100.table_ref = bf16[256,768]{1,0:T(8,128)(2,1)S(1)} custom-call(bf16[256,1024]{1,0:T(8,128)(2,1)} %table_hbm.1, bf16[1024,256]{1,0:T(8,128)(2,1)} %wq_hbm.1, bf16[1024,256]{1,0:T(8,128)(2,1)} %wk_hbm.1, bf16[1024,256]{1,0:T(8,128)(2,1)} %wv_hbm.1), custom_call_target="tpu_custom_call" | custom-call | tf_op jit(solution)/shard_map/pallas_call | solution.py:248
  7.1 0.0 copy-start
  7.1 0.0 copy-start.1
  7.2 0.0 copy-start.2
  7.2 0.0 copy-done.3
  7.2 0.0 copy-done.4
  7.2 0.3 shard_map.101
  7.5 1.5 %collective-permute-done = s32[192]{0:T(256)S(1)} collective-permute-done((s32[192]{0:T(256)}, s32[192]{0:T(256)S(1)}, u32[]{:S(2)}, u32[]{:S(2)}) %collective-permute-start) | collective-permute-done | bytes 800 | tf_op jit(solution)/shard_map/ppermute | solution.py:281
  9.0 1.4 %shard_map.102 = (bf16[192,256]{1,0:T(8,128)(2,1)S(1)}, bf16[16,72,256]{2,1,0:T(8,128)(2,1)S(1)}) custom-call(s32[1]{0:T(128)} %bitcast.2.block_ref, s32[1,192]{1,0:T(1,128)S(1)} %bitcast.10, bf16[256,768]{1,0:T(8,128)(2,1)S(1)} %shard_map.100.table_ref, bf16[192,768]{1,0:T(8,128)(2,1)S(1)} %get-tuple-element.16.own_ref, ...), custom_call_target="tpu_custom_call" | custom-call | tf_op jit(solution)/shard_map/pallas_call | solution.py:248
  10.4 17.8 %all_to_all.10.own_ref = bf16[16,72,256]{2,1,0:T(8,128)(2,1)S(1)} all-to-all(bf16[16,72,256]{2,1,0:T(8,128)(2,1)S(1)} %get-tuple-element.18), channel_id=1, replica_groups=mesh['bytes'=16,'x'=4,'core'=2,'tp'=4] {'x','tp'}, dimensions={0} | all-to-all | bytes 1179648 | tf_op jit(solution)/shard_map/all_to_all | solution.py:267
  28.1 2.3 %collective-permute-start.1 = (bf16[16,72,256]{2,1,0:T(8,128)(2,1)S(1)}, bf16[16,72,256]{2,1,0:T(8,128)(2,1)S(1)}, u32[]{:S(2)}, u32[]{:S(2)}) collective-permute-start(bf16[16,72,256]{2,1,0:T(8,128)(2,1)S(1)} %all_to_all.10.own_ref), channel_id=1, source_target_pairs={{0,4},{4,0},{1,5},{5,1},{2,6},{6,2},{3,7},{7,3},{8,12},{12,8},{9,1... | collective-permute-start | bytes 1769480 | tf_op jit(solution)/shard_map/ppermute | solution.py:263
  30.5 0.0 copy-done
  30.5 0.0 copy-done.1
  30.5 0.0 copy-done.2
  30.5 0.8 shard_map.103
  31.3 0.8 collective-permute-done.1.other_ref
  32.1 1.2 %shard_map.104 = (bf16[384,128]{1,0:T(8,128)(2,1)S(1)}, bf16[392,256]{1,0:T(8,128)(2,1)S(1)}, s32[8,576]{1,0:T(8,128)S(1)}) custom-call(s32[1]{0:T(128)} %bitcast.1.core_ref, bf16[288,384]{1,0:T(8,128)(2,1)S(1)} %get-tuple-element.19.made_ref, f32[8,128]{1,0:T(8,128)S(1)} %get-tuple-element.20.count_ref, ...), custom_call_target="tpu_custom_call" | custom-call | tf_op jit(solution)/shard_map/pallas_call | solution.py:248
  33.4 52.4 %all-gather.1 = f16[6272,256]{1,0:T(8,128)(2,1)S(1)} all-gather(f16[392,256]{1,0:T(8,128)(2,1)S(1)} %convert_element_type.15), channel_id=1, replica_groups=mesh['bytes'=16,'x'=4,'core'=2,'tp'=4] {'bytes'}, dimensions={0}, use_global_device_ids=true | all-gather | bytes 3411968 | tf_op jit(solution)/shard_map/all_gather | solution.py:272
  85.8 0.7 convert_element_type.16
  86.5 1.6 %shard_map.105 = (bf16[384,128]{1,0:T(8,128)(2,1)S(1)}, bf16[16,72,256]{2,1,0:T(8,128)(2,1)S(1)}) custom-call(s32[1]{0:T(128)} %bitcast.z_ref, bf16[384,128]{1,0:T(8,128)(2,1)S(1)} %get-tuple-element.21.q_ref, bf16[16,392,256]{2,1,0:T(8,128)(2,1)S(1)} %bitcast.7, s32[8,576]{1,0:T(8,128)S(1)} %get-tuple-element.23.place_ref, bf16[128,1024]{1,0:T(8,128)(2,1)} %w_ref.1), custom_call_target="tpu_custom_call" | custom-call | tf_op jit(solution)/shard_map/pallas_call | solution.py:248
  88.1 9.2 %collective-permute-start.2 = (bf16[16,72,256]{2,1,0:T(8,128)(2,1)S(1)}, bf16[16,72,256]{2,1,0:T(8,128)(2,1)S(1)}, u32[]{:S(2)}, u32[]{:S(2)}) collective-permute-start(bf16[16,72,256]{2,1,0:T(8,128)(2,1)S(1)} %get-tuple-element.25), channel_id=1, source_target_pairs={{0,4},{4,0},{1,5},{5,1},{2,6},{6,2},{3,7},{7,3},{8,12},{12,8},{9,1... | collective-permute-start | bytes 1769480 | tf_op jit(solution)/shard_map/ppermute | solution.py:263
  97.2 1.5 %shard_map.106 = bf16[16,72,256]{2,1,0:T(8,128)(2,1)S(1)} custom-call(bf16[384,128]{1,0:T(8,128)(2,1)S(1)} %get-tuple-element.24.mixed_ref, s32[8,576]{1,0:T(8,128)S(1)} %get-tuple-element.23.place_ref, bf16[128,1024]{1,0:T(8,128)(2,1)} %w_ref.1), custom_call_target="tpu_custom_call" | custom-call | tf_op jit(solution)/shard_map/pallas_call | solution.py:248
  98.7 0.1 collective-permute-done.2
  98.8 0.2 add_convert_fusion
  99.0 14.6 %all_to_all.11.got_ref = bf16[16,72,256]{2,1,0:T(8,128)(2,1)S(1)} all-to-all(bf16[16,72,256]{2,1,0:T(8,128)(2,1)S(1)} %add_convert_fusion), channel_id=1, replica_groups=mesh['bytes'=16,'x'=4,'core'=2,'tp'=4] {'x','tp'}, dimensions={0} | all-to-all | bytes 1179648 | tf_op jit(solution)/shard_map/all_to_all | solution.py:267
  113.6 0.9 shard_map.107
  (1 shorter events, 0.0 us)
Async XLA Ops:
  0.0 9.0 %collective-permute-start = (s32[192]{0:T(256)}, s32[192]{0:T(256)S(1)}, u32[]{:S(2)}, u32[]{:S(2)}) collective-permute-start(s32[192]{0:T(256)} %param.10), channel_id=1, source_target_pairs={{0,4},{4,8},{8,12},{12,16},{16,20},{20,24},{24,28},{28,32},{32,36}... | collective-permute-start | bytes 2312 | tf_op jit(solution)/shard_map/ppermute | solution.py:281
  4.5 2.7 %copy-start.3 = (s32[192]{0:T(256)S(1)}, s32[192]{0:T(256)}, u32[]{:S(2)}) copy-start(s32[192]{0:T(256)} %param.11) | copy-start | bytes 2308
  4.5 2.7 %copy-start.4 = (s32[192]{0:T(256)S(1)}, s32[192]{0:T(256)}, u32[]{:S(2)}) copy-start(s32[192]{0:T(256)} %param.10) | copy-start | bytes 2308
  7.1 23.4 %copy-start = (bf16[1024,128]{1,0:T(8,128)(2,1)S(1)}, bf16[1024,128]{1,0:T(8,128)(2,1)}, u32[]{:S(2)}) copy-start(bf16[1024,128]{1,0:T(8,128)(2,1)} %wq_ref.3) | copy-start | bytes 786436
  7.1 23.4 %copy-start.1 = (bf16[1024,128]{1,0:T(8,128)(2,1)S(1)}, bf16[1024,128]{1,0:T(8,128)(2,1)}, u32[]{:S(2)}) copy-start(bf16[1024,128]{1,0:T(8,128)(2,1)} %wk_ref.3) | copy-start | bytes 786436
  7.2 23.4 %copy-start.2 = (bf16[1024,128]{1,0:T(8,128)(2,1)S(1)}, bf16[1024,128]{1,0:T(8,128)(2,1)}, u32[]{:S(2)}) copy-start(bf16[1024,128]{1,0:T(8,128)(2,1)} %wv_ref.3) | copy-start | bytes 786436
  28.1 4.0 %collective-permute-start.1 = (bf16[16,72,256]{2,1,0:T(8,128)(2,1)S(1)}, bf16[16,72,256]{2,1,0:T(8,128)(2,1)S(1)}, u32[]{:S(2)}, u32[]{:S(2)}) collective-permute-start(bf16[16,72,256]{2,1,0:T(8,128)(2,1)S(1)} %all_to_all.10.own_ref), channel_id=1, source_target_pairs={{0,4},{4,0},{1,5},{5,1},{2,6},{6,2},{3,7},{7,3},{8,12},{12,8},{9,1... | collective-permute-start | bytes 1769480 | tf_op jit(solution)/shard_map/ppermute | solution.py:263
  88.1 10.8 %collective-permute-start.2 = (bf16[16,72,256]{2,1,0:T(8,128)(2,1)S(1)}, bf16[16,72,256]{2,1,0:T(8,128)(2,1)S(1)}, u32[]{:S(2)}, u32[]{:S(2)}) collective-permute-start(bf16[16,72,256]{2,1,0:T(8,128)(2,1)S(1)} %get-tuple-element.25), channel_id=1, source_target_pairs={{0,4},{4,0},{1,5},{5,1},{2,6},{6,2},{3,7},{7,3},{8,12},{12,8},{9,1... | collective-permute-start | bytes 1769480 | tf_op jit(solution)/shard_map/ppermute | solution.py:263

commit v5 on v4

--- a/solution.py
+++ b/solution.py
@@ -15,7 +15,7 @@
 UNUSED = 1e9
 GROUP = 384
 KVROWS = 392
-SPANS = (1, 3, 4, 4, 4)
+SPANS = (1, 2, 4, 4, 5)
 EPSILON = 1e-06
 NEGATIVE = -1e30
 F32 = jnp.float32
@@ -103,7 +103,7 @@
         scores = jnp.where(allowed, scores, NEGATIVE)
         weights = jnp.exp(scores - jnp.max(scores, axis=-1, keepdims=True))
         totals = jnp.sum(weights, axis=-1, keepdims=True)
-        encoded = encoded + dot(weights.astype(BF16), values * mine) / totals
+        encoded = encoded + dot(weights.astype(BF16), values * mine) * (1.0 / totals)
     encoded = encoded.astype(BF16)
     enc_ref[...] = encoded
     members = member_ref[...]
@@ -238,8 +238,9 @@
         decoded = decoded + got_ref[h].astype(F32)
     high = decoded.astype(BF16)
     low = (decoded - high.astype(F32)).astype(BF16)
-    members = member_ref[...]
-    out_ref[...] = (enc_ref[...].astype(F32) + dot_tn(members, high) + dot_tn(members, low)).astype(BF16)
+    members = jnp.concatenate([member_ref[...], member_ref[...]], axis=0)
+    both = jnp.concatenate([high, low], axis=0)
+    out_ref[...] = (enc_ref[...].astype(F32) + dot_tn(members, both)).astype(BF16)
 
 
 def call(kernel, shapes, specs, *args, scratch=(), grant=16):

time: 115 us -> 115 us (level)
  no operation moved by 1% of the time
where the time goes in v5:
time: 115 us; the launch traced here: 114 us
  blocking collectives  84.8 us (74%)
  starting transfers between devices  16 us (14%)
  Pallas kernels  10.2 us (9%)
  waiting for transfers between devices  2.44 us (2%)
    all_gather x1, blocking collectives, gather_keys(): got = lax.all_gather(kv.astype(jnp.float16), 'bytes', axis=0, tiled=True)  52.4 us
    all_to_all x2, blocking collectives, exchange(): lax.all_to_all(value, ('x', 'tp'), split_axis=0, concat_axis=0, tiled=True)  32.4 us
    ppermute x2, starting transfers between devices, swap_cores(): return lax.ppermute(value, 'core', [(0, 1), (1, 0)])  11.5 us
    pallas_call x8, Pallas kernels, call(): pl.pallas_call(kernel, out_shape=structs[0] if single else structs, in_sp...  10.2 us
    ppermute x1, starting transfers between devices, per_device(): lax.ppermute(ids, ring, [(i, i + 1) for i in range(lax.axis_size(ring) -...  4.49 us
  transfers between devices with their start and end apart: 3, of which 3 were waited for; matrix products, arithmetic and copies ran while one was open for 0% of the time, Pallas kernels for 4%

profile of v5, /device:TPU:1, one launch (start us, length us, event | category | flops | bytes accessed | tf_op | source)
XLA Modules:
  0.0 114.5 jit_solution(10670199810250796119)
XLA Ops:
  0.0 4.5 %collective-permute-start = (s32[192]{0:T(256)}, s32[192]{0:T(256)S(1)}, u32[]{:S(2)}, u32[]{:S(2)}) collective-permute-start(s32[192]{0:T(256)} %param.10), channel_id=1, source_target_pairs={{0,4},{4,8},{8,12},{12,16},{16,20},{20,24},{24,28},{28,32},{32,36}... | collective-permute-start | bytes 2312 | tf_op jit(solution)/shard_map/ppermute | solution.py:282
  4.5 0.0 copy-start.3
  4.5 0.0 copy-start.4
  4.5 2.6 %shard_map.100.table_ref = bf16[256,768]{1,0:T(8,128)(2,1)S(1)} custom-call(bf16[256,1024]{1,0:T(8,128)(2,1)} %table_hbm.1, bf16[1024,256]{1,0:T(8,128)(2,1)} %wq_hbm.1, bf16[1024,256]{1,0:T(8,128)(2,1)} %wk_hbm.1, bf16[1024,256]{1,0:T(8,128)(2,1)} %wv_hbm.1), custom_call_target="tpu_custom_call" | custom-call | tf_op jit(solution)/shard_map/pallas_call | solution.py:249
  7.1 0.0 copy-start
  7.1 0.0 copy-start.1
  7.2 0.0 copy-start.2
  7.2 0.0 copy-done.3
  7.2 0.0 copy-done.4
  7.2 0.3 shard_map.101
  7.5 1.5 %collective-permute-done = s32[192]{0:T(256)S(1)} collective-permute-done((s32[192]{0:T(256)}, s32[192]{0:T(256)S(1)}, u32[]{:S(2)}, u32[]{:S(2)}) %collective-permute-start) | collective-permute-done | bytes 800 | tf_op jit(solution)/shard_map/ppermute | solution.py:282
  9.0 1.4 %shard_map.102 = (bf16[192,256]{1,0:T(8,128)(2,1)S(1)}, bf16[16,72,256]{2,1,0:T(8,128)(2,1)S(1)}) custom-call(s32[1]{0:T(128)} %bitcast.2.block_ref, s32[1,192]{1,0:T(1,128)S(1)} %bitcast.10, bf16[256,768]{1,0:T(8,128)(2,1)S(1)} %shard_map.100.table_ref, bf16[192,768]{1,0:T(8,128)(2,1)S(1)} %get-tuple-element.16.own_ref, ...), custom_call_target="tpu_custom_call" | custom-call | tf_op jit(solution)/shard_map/pallas_call | solution.py:249
  10.4 17.8 %all_to_all.10.own_ref = bf16[16,72,256]{2,1,0:T(8,128)(2,1)S(1)} all-to-all(bf16[16,72,256]{2,1,0:T(8,128)(2,1)S(1)} %get-tuple-element.18), channel_id=1, replica_groups=mesh['bytes'=16,'x'=4,'core'=2,'tp'=4] {'x','tp'}, dimensions={0} | all-to-all | bytes 1179648 | tf_op jit(solution)/shard_map/all_to_all | solution.py:268
  28.1 2.3 %collective-permute-start.1 = (bf16[16,72,256]{2,1,0:T(8,128)(2,1)S(1)}, bf16[16,72,256]{2,1,0:T(8,128)(2,1)S(1)}, u32[]{:S(2)}, u32[]{:S(2)}) collective-permute-start(bf16[16,72,256]{2,1,0:T(8,128)(2,1)S(1)} %all_to_all.10.own_ref), channel_id=1, source_target_pairs={{0,4},{4,0},{1,5},{5,1},{2,6},{6,2},{3,7},{7,3},{8,12},{12,8},{9,1... | collective-permute-start | bytes 1769480 | tf_op jit(solution)/shard_map/ppermute | solution.py:264
  30.5 0.0 copy-done
  30.5 0.0 copy-done.1
  30.5 0.0 copy-done.2
  30.5 0.8 shard_map.103
  31.3 0.8 collective-permute-done.1.other_ref
  32.1 1.2 %shard_map.104 = (bf16[384,128]{1,0:T(8,128)(2,1)S(1)}, bf16[392,256]{1,0:T(8,128)(2,1)S(1)}, s32[8,576]{1,0:T(8,128)S(1)}) custom-call(s32[1]{0:T(128)} %bitcast.1.core_ref, bf16[288,384]{1,0:T(8,128)(2,1)S(1)} %get-tuple-element.19.made_ref, f32[8,128]{1,0:T(8,128)S(1)} %get-tuple-element.20.count_ref, ...), custom_call_target="tpu_custom_call" | custom-call | tf_op jit(solution)/shard_map/pallas_call | solution.py:249
  33.4 52.4 %all-gather.1 = f16[6272,256]{1,0:T(8,128)(2,1)S(1)} all-gather(f16[392,256]{1,0:T(8,128)(2,1)S(1)} %convert_element_type.15), channel_id=1, replica_groups=mesh['bytes'=16,'x'=4,'core'=2,'tp'=4] {'bytes'}, dimensions={0}, use_global_device_ids=true | all-gather | bytes 3411968 | tf_op jit(solution)/shard_map/all_gather | solution.py:273
  85.8 0.7 convert_element_type.16
  86.5 1.6 %shard_map.105 = (bf16[384,128]{1,0:T(8,128)(2,1)S(1)}, bf16[16,72,256]{2,1,0:T(8,128)(2,1)S(1)}) custom-call(s32[1]{0:T(128)} %bitcast.z_ref, bf16[384,128]{1,0:T(8,128)(2,1)S(1)} %get-tuple-element.21.q_ref, bf16[16,392,256]{2,1,0:T(8,128)(2,1)S(1)} %bitcast.7, s32[8,576]{1,0:T(8,128)S(1)} %get-tuple-element.23.place_ref, bf16[128,1024]{1,0:T(8,128)(2,1)} %w_ref.1), custom_call_target="tpu_custom_call" | custom-call | tf_op jit(solution)/shard_map/pallas_call | solution.py:249
  88.1 9.2 %collective-permute-start.2 = (bf16[16,72,256]{2,1,0:T(8,128)(2,1)S(1)}, bf16[16,72,256]{2,1,0:T(8,128)(2,1)S(1)}, u32[]{:S(2)}, u32[]{:S(2)}) collective-permute-start(bf16[16,72,256]{2,1,0:T(8,128)(2,1)S(1)} %get-tuple-element.25), channel_id=1, source_target_pairs={{0,4},{4,0},{1,5},{5,1},{2,6},{6,2},{3,7},{7,3},{8,12},{12,8},{9,1... | collective-permute-start | bytes 1769480 | tf_op jit(solution)/shard_map/ppermute | solution.py:264
  97.2 1.5 %shard_map.106 = bf16[16,72,256]{2,1,0:T(8,128)(2,1)S(1)} custom-call(bf16[384,128]{1,0:T(8,128)(2,1)S(1)} %get-tuple-element.24.mixed_ref, s32[8,576]{1,0:T(8,128)S(1)} %get-tuple-element.23.place_ref, bf16[128,1024]{1,0:T(8,128)(2,1)} %w_ref.1), custom_call_target="tpu_custom_call" | custom-call | tf_op jit(solution)/shard_map/pallas_call | solution.py:249
  98.7 0.1 collective-permute-done.2
  98.8 0.2 add_convert_fusion
  99.0 14.6 %all_to_all.11.got_ref = bf16[16,72,256]{2,1,0:T(8,128)(2,1)S(1)} all-to-all(bf16[16,72,256]{2,1,0:T(8,128)(2,1)S(1)} %add_convert_fusion), channel_id=1, replica_groups=mesh['bytes'=16,'x'=4,'core'=2,'tp'=4] {'x','tp'}, dimensions={0} | all-to-all | bytes 1179648 | tf_op jit(solution)/shard_map/all_to_all | solution.py:268
  113.6 0.9 shard_map.107
  (1 shorter events, 0.0 us)
Async XLA Ops:
  0.0 9.0 %collective-permute-start = (s32[192]{0:T(256)}, s32[192]{0:T(256)S(1)}, u32[]{:S(2)}, u32[]{:S(2)}) collective-permute-start(s32[192]{0:T(256)} %param.10), channel_id=1, source_target_pairs={{0,4},{4,8},{8,12},{12,16},{16,20},{20,24},{24,28},{28,32},{32,36}... | collective-permute-start | bytes 2312 | tf_op jit(solution)/shard_map/ppermute | solution.py:282
  4.5 2.7 %copy-start.3 = (s32[192]{0:T(256)S(1)}, s32[192]{0:T(256)}, u32[]{:S(2)}) copy-start(s32[192]{0:T(256)} %param.11) | copy-start | bytes 2308
  4.5 2.7 %copy-start.4 = (s32[192]{0:T(256)S(1)}, s32[192]{0:T(256)}, u32[]{:S(2)}) copy-start(s32[192]{0:T(256)} %param.10) | copy-start | bytes 2308
  7.1 23.4 %copy-start = (bf16[1024,128]{1,0:T(8,128)(2,1)S(1)}, bf16[1024,128]{1,0:T(8,128)(2,1)}, u32[]{:S(2)}) copy-start(bf16[1024,128]{1,0:T(8,128)(2,1)} %wq_ref.3) | copy-start | bytes 786436
  7.1 23.4 %copy-start.1 = (bf16[1024,128]{1,0:T(8,128)(2,1)S(1)}, bf16[1024,128]{1,0:T(8,128)(2,1)}, u32[]{:S(2)}) copy-start(bf16[1024,128]{1,0:T(8,128)(2,1)} %wk_ref.3) | copy-start | bytes 786436
  7.2 23.4 %copy-start.2 = (bf16[1024,128]{1,0:T(8,128)(2,1)S(1)}, bf16[1024,128]{1,0:T(8,128)(2,1)}, u32[]{:S(2)}) copy-start(bf16[1024,128]{1,0:T(8,128)(2,1)} %wv_ref.3) | copy-start | bytes 786436
  28.1 4.0 %collective-permute-start.1 = (bf16[16,72,256]{2,1,0:T(8,128)(2,1)S(1)}, bf16[16,72,256]{2,1,0:T(8,128)(2,1)S(1)}, u32[]{:S(2)}, u32[]{:S(2)}) collective-permute-start(bf16[16,72,256]{2,1,0:T(8,128)(2,1)S(1)} %all_to_all.10.own_ref), channel_id=1, source_target_pairs={{0,4},{4,0},{1,5},{5,1},{2,6},{6,2},{3,7},{7,3},{8,12},{12,8},{9,1... | collective-permute-start | bytes 1769480 | tf_op jit(solution)/shard_map/ppermute | solution.py:264
  88.1 10.8 %collective-permute-start.2 = (bf16[16,72,256]{2,1,0:T(8,128)(2,1)S(1)}, bf16[16,72,256]{2,1,0:T(8,128)(2,1)S(1)}, u32[]{:S(2)}, u32[]{:S(2)}) collective-permute-start(bf16[16,72,256]{2,1,0:T(8,128)(2,1)S(1)} %get-tuple-element.25), channel_id=1, source_target_pairs={{0,4},{4,0},{1,5},{5,1},{2,6},{6,2},{3,7},{7,3},{8,12},{12,8},{9,1... | collective-permute-start | bytes 1769480 | tf_op jit(solution)/shard_map/ppermute | solution.py:264
